TPU v7x, 32 devices: a whole 2x2x4 slice. The times are simulated.
32 devices in a mesh: wide: 8 (over z, y), narrow: 4 (over x, core).
Axes of the slice: x: 2, y: 2, z: 4, core: 2. Of those that a mesh axis runs over, the one named last changes fastest.
Arguments:
- values: float32 [512, 16384], P(('wide', 'narrow')), may hold values from -200 to 200, as said below
- cloud_words: int32 [512, 512], P(('wide', 'narrow')), may hold values from -2147483648 to 2147483647, as said below
- history_len: int32 [1], replicated, may hold values from 96 to 256
- monitor_start: int32 [1], replicated, may hold values from 256 to 384
- boundary_table: int32 [512], replicated, may hold values from 500 to 2000
Outputs:
- ratio: float32 [512, 16384], P(('wide', 'narrow'))
- peak_so_far: float32 [512, 16384], P(('wide', 'narrow'))
Inputs may be any that keep to these rules, and one draw needn't show every extreme that they name: `values`: values of an index series, mixed noise and a seasonal cycle of varying scale. `cloud_words`: bit b of word j in the row of date t is 1 when pixel 32 j + b is clear at date t; the first 16 dates are clear for every pixel.
All inputs are finite; a program needn't handle non-finite values.
Results may differ from a plain program's by a relative error of at most 0.0003.
Values sent between devices are 32-bit elements; how exact they have to be, the bound alone decides.
A program may use at most 64 MiB of HBM per device.

v0:
```python
import functools
import math

import jax
import jax.numpy as jnp
from jax import lax
from jax.experimental import pallas as pl
from jax.experimental.pallas import tpu as pltpu
import numpy as np
from jax.sharding import PartitionSpec as P

PERIOD = 46
HARMONICS = 3
COLS = 8
WINDOW = 64


HIGH = lax.Precision.HIGHEST


def unpack_clear(words):
    shifts = jnp.arange(32, dtype=jnp.int32)
    flags = jnp.bitwise_and(jnp.right_shift(words[:, :, None], shifts[None, None, :]), jnp.int32(1))
    return flags.reshape(words.shape[0], words.shape[1] * 32).astype(jnp.float32)


def harmonic_design(dates):
    day_float = jnp.arange(dates, dtype=jnp.int32).astype(jnp.float32)
    columns = [jnp.ones((dates,), jnp.float32), day_float / dates]
    for harmonic in range(1, HARMONICS + 1):
        phases = 2.0 * math.pi * harmonic / PERIOD * day_float
        columns.append(jnp.cos(phases))
        columns.append(jnp.sin(phases))
    return jnp.stack(columns, axis=1)


def solve_batched(normal_mat, target):
    size_cols = normal_mat.shape[0]
    factor = [[None] * size_cols for row_idx in range(size_cols)]
    for row_idx in range(size_cols):
        for col_idx in range(row_idx + 1):
            summed = normal_mat[row_idx, col_idx]
            for mid_idx in range(col_idx):
                summed = summed - factor[row_idx][mid_idx] * factor[col_idx][mid_idx]
            if row_idx == col_idx:
                factor[row_idx][col_idx] = jnp.sqrt(summed)
            else:
                factor[row_idx][col_idx] = summed / factor[col_idx][col_idx]
    forward = []
    for row_idx in range(size_cols):
        summed = target[row_idx]
        for mid_idx in range(row_idx):
            summed = summed - factor[row_idx][mid_idx] * forward[mid_idx]
        forward.append(summed / factor[row_idx][row_idx])
    solution = [None] * size_cols
    for row_idx in reversed(range(size_cols)):
        summed = forward[row_idx]
        for mid_idx in range(row_idx + 1, size_cols):
            summed = summed - factor[mid_idx][row_idx] * solution[mid_idx]
        solution[row_idx] = summed / factor[row_idx][row_idx]
    return jnp.stack(solution, axis=0)


def fit_statistic(values, clear, history_len, monitor_start, boundary_table):
    dates = values.shape[0]
    day = jnp.arange(dates, dtype=jnp.int32)
    design = harmonic_design(dates)
    in_history = (day < history_len[0]).astype(jnp.float32)[:, None]
    weight = clear * in_history
    outer = (design[:, :, None] * design[:, None, :]).reshape(dates, COLS * COLS)
    normal_mat = jnp.dot(
        outer.T, weight, precision=HIGH, preferred_element_type=jnp.float32
    ).reshape(COLS, COLS, -1)
    target = jnp.dot(design.T, weight * values, precision=HIGH, preferred_element_type=jnp.float32)
    coeffs = solve_batched(normal_mat, target)
    fitted = jnp.dot(design, coeffs, precision=HIGH, preferred_element_type=jnp.float32)
    resid = clear * (values - fitted)
    count = jnp.sum(weight, axis=0)
    squares = jnp.sum(weight * resid * resid, axis=0)
    sigma = jnp.sqrt(squares / (count - COLS) + 1e-06)
    lagged = day[:, None] - day[None, :]
    banded = ((lagged >= 0) & (lagged < WINDOW)).astype(jnp.float32)
    moving = jnp.dot(banded, resid, precision=HIGH, preferred_element_type=jnp.float32)
    scaled = moving / (sigma * jnp.sqrt(count))[None, :]
    bounds = boundary_table.astype(jnp.float32) * 0.001
    watching = (day >= monitor_start[0])[:, None]
    return jnp.where(watching, scaled / bounds[:, None], jnp.float32(0.0))


def per_device(values, cloud_words, history_len, monitor_start, boundary_table):
    arrived = lax.all_to_all(values, ("wide", "narrow"), split_axis=1, concat_axis=0, tiled=True)
    words = lax.all_to_all(cloud_words, ("wide", "narrow"), split_axis=1, concat_axis=0, tiled=True)
    ratio = fit_statistic(arrived, unpack_clear(words), history_len, monitor_start, boundary_table)
    rows = values.shape[0]
    blocks = ratio.reshape(ratio.shape[0] // rows, rows, ratio.shape[1])
    block_peak = lax.cummax(jnp.max(jnp.abs(blocks), axis=1), axis=0)
    earlier = jnp.concatenate([jnp.zeros_like(block_peak[:1]), block_peak[:-1]], axis=0)
    date_ratio = lax.all_to_all(ratio, ("wide", "narrow"), split_axis=0, concat_axis=1, tiled=True)
    before = lax.all_to_all(earlier, ("wide", "narrow"), split_axis=0, concat_axis=1, tiled=True)
    peak = jnp.maximum(lax.cummax(jnp.abs(date_ratio), axis=0), before)
    return (date_ratio, peak)


HISTORY_MOST = 256
MESH = pl.DeviceIdType.MESH


def host_design(dates):
    day = np.arange(dates, dtype=np.float32)
    columns = [np.ones((dates,), np.float32), (day / np.float32(dates)).astype(np.float32)]
    for harmonic in range(1, HARMONICS + 1):
        phases = (np.float32(2.0 * math.pi * harmonic / PERIOD) * day).astype(np.float64)
        columns.append(np.cos(phases).astype(np.float32))
        columns.append(np.sin(phases).astype(np.float32))
    return np.stack(columns, axis=1)


def dot_high(left, right):
    return jnp.dot(left, right, precision=HIGH, preferred_element_type=jnp.float32)


def clear_bits(words, offset, pixels):
    rows, lanes = words.shape
    parts = [((words >> (8 * k)) & 255).astype(jnp.float32).astype(jnp.bfloat16) for k in range(4)]
    stacked = jnp.concatenate(parts, axis=0)
    word_of = lax.broadcasted_iota(jnp.int32, (lanes, pixels), 1) >> 5
    spread = (lax.broadcasted_iota(jnp.int32, (lanes, pixels), 0) - offset == word_of)
    spread = spread.astype(jnp.float32).astype(jnp.bfloat16)
    wide = jnp.dot(stacked, spread, preferred_element_type=jnp.float32)
    lane = lax.broadcasted_iota(jnp.int32, (rows, pixels), 1)
    which = (lane >> 3) & 3
    byte = wide[:rows]
    for k in range(1, 4):
        byte = jnp.where(which == k, wide[k * rows : (k + 1) * rows], byte)
    return ((byte.astype(jnp.int32) >> (lane & 7)) & 1).astype(jnp.float32)


def scan_rows(array, combine, neutral):
    tiles = []
    row = lax.broadcasted_iota(jnp.int32, (8, array.shape[1]), 0)
    for at in range(0, array.shape[0], 8):
        tile = array[at : at + 8]
        for step in (1, 2, 4):
            tile = combine(tile, jnp.where(row >= step, pltpu.roll(tile, step, 0), neutral))
        if tiles:
            tile = combine(tile, tiles[-1][7:8])
        tiles.append(tile)
    return jnp.concatenate(tiles, axis=0)


def fitted(design, coeffs):
    total = design[:, 0:1] * coeffs[0:1]
    for k in range(1, COLS):
        total = total + design[:, k : k + 1] * coeffs[k : k + 1]
    return total


def solve_rows(entry, target):
    factor = [[None] * COLS for _ in range(COLS)]
    inverse = [None] * COLS
    for i in range(COLS):
        for j in range(i + 1):
            summed = entry(i, j)
            for m in range(j):
                summed = summed - factor[i][m] * factor[j][m]
            if i == j:
                inverse[i] = 1.0 / jnp.sqrt(summed)
            else:
                factor[i][j] = summed * inverse[j]
    forward = []
    for i in range(COLS):
        summed = target(i)
        for m in range(i):
            summed = summed - factor[i][m] * forward[m]
        forward.append(summed * inverse[i])
    answer = [None] * COLS
    for i in reversed(range(COLS)):
        summed = forward[i]
        for m in range(i + 1, COLS):
            summed = summed - factor[m][i] * answer[m]
        answer[i] = summed * inverse[i]
    return answer


def fused_kernel(
    narrow, chips, hist, back,
    hl_ref, ms_ref, b_ref, v_ref, w_ref, d_hbm, ot_hbm, ratio_ref, peak_ref,
    cv, cw, ccl, hv, hw, ow, tp, tb, nm, cb, cnt, sq, sb, tot, tt, sc, scb, rt, mrow, mb, rin, pin, dm, de, ot_ref,
    ax_s, ax_r, ha_s, ha_r, hw_s, hw_r, ow_s, ow_r, tp_s, tp_r, cb_s, cb_r, ct_s, ct_r,
    sq_s, sq_r, tt_s, tt_r, sc_s, sc_r, mx_s, mx_r, or_s, or_r, op_s, op_r, lc,
):
    me = lax.axis_index("wide") * narrow + lax.axis_index("narrow")
    q, c = lax.div(me, 2), lax.rem(me, 2)
    rows, pixels = v_ref.shape
    half = pixels // 2
    own = half // hist
    slots = hist
    chip_rows = 2 * rows
    late = chips - hist
    is_hist = q < hist
    is_late = q >= hist

    def dev(q2, c2):
        d = 2 * q2 + c2
        return (lax.div(d, narrow), lax.rem(d, narrow))

    def remote(src, dst, ssem, rsem, q2, c2):
        return pltpu.make_async_remote_copy(
            src_ref=src, dst_ref=dst, send_sem=ssem, recv_sem=rsem,
            device_id=dev(q2, c2), device_id_type=MESH)

    def cols(s):
        return pl.ds(pl.multiple_of(s * own, own), own)

    mine = pl.ds(pl.multiple_of(c * rows, rows), rows)
    theirs = pl.ds(pl.multiple_of((1 - c) * rows, rows), rows)
    my_half = pl.ds(pl.multiple_of(c * half, half), half)
    other_half = pl.ds(pl.multiple_of((1 - c) * half, half), half)

    def half_col(h, s):
        return pl.ds(pl.multiple_of(h * half + s * own, own), own)

    swap_v = remote(v_ref.at[:, other_half], cv.at[mine, :], ax_s.at[0], ax_r.at[0], q, 1 - c)
    swap_w = remote(w_ref, cw.at[mine, :], ax_s.at[1], ax_r.at[1], q, 1 - c)
    swap_w.start()
    swap_v.start()
    get_d = pltpu.make_async_copy(d_hbm.at[q], dm, lc.at[3])
    get_e = pltpu.make_async_copy(d_hbm.at[lax.max(q - back, 0)], de, lc.at[4])
    get_o = pltpu.make_async_copy(ot_hbm, ot_ref, lc.at[5])
    get_d.start()
    get_e.start()
    get_o.start()
    keep_v = pltpu.make_async_copy(v_ref.at[:, my_half], cv.at[mine, :], lc.at[0])
    keep_w = pltpu.make_async_copy(w_ref, cw.at[mine, :], lc.at[1])
    keep_v.start()
    keep_w.start()

    def owner_block(q2, c2):
        return pl.ds(pl.multiple_of(lax.div(c2 * half + q2 * own, 32 * 128) * 128, 128), 128)

    my_dates = pl.ds(pl.multiple_of(me * rows, rows), rows)
    keep_o = pltpu.make_async_copy(w_ref.at[:, owner_block(q, c)], ow.at[my_dates, :], lc.at[2])

    def send_words(k):
        to = lax.rem(me + k, 2 * hist)
        return remote(w_ref.at[:, owner_block(lax.div(to, 2), lax.rem(to, 2))],
                      ow.at[my_dates, :], ow_s.at[k - 1], ow_r.at[k - 1],
                      lax.div(to, 2), lax.rem(to, 2))

    @pl.when(is_hist)
    def _():
        @pl.loop(1, 2 * hist)
        def _(k):
            send_words(k).start()
        keep_o.start()

    sends_early = jnp.logical_and(q + back >= hist, q + back < chips)

    def early_words(h):
        return remote(w_ref, hw.at[mine, :], hw_s.at[h], hw_r.at[c], q + back, h)

    def early(h, s):
        return remote(v_ref.at[:, half_col(h, s)], hv.at[mine, cols(s)],
                      ha_s.at[h * slots + s], ha_r.at[c * slots + s], q + back, h)

    third, most = slots // 4, slots * 5 // 8

    def start_early(low, high):
        @pl.when(sends_early)
        def _():
            @pl.loop(low, high)
            def _(s):
                early(0, s).start()
                early(1, s).start()

    @pl.when(sends_early)
    def _():
        for h in range(2):
            early_words(h).start()

    start_early(0, third)

    @pl.when(is_late)
    def _():
        start_early(third, most)

    def word_block(s):
        start = c * (half // 32) + s * (own // 32)
        base = lax.div(start, 128) * 128
        return pl.ds(pl.multiple_of(base, 128), 128), start - base

    keep_w.wait()
    swap_w.wait_recv()

    @pl.loop(0, slots)
    def _(s):
        block, offset = word_block(s)
        ccl[:, cols(s)] = clear_bits(cw[:, block], offset, own)

    keep_v.wait()
    swap_v.wait_recv()
    get_d.wait()
    get_e.wait()
    get_o.wait()
    date = q * chip_rows + lax.broadcasted_iota(jnp.int32, (chip_rows, own), 0)

    def send_target(k):
        to = lax.rem(q + k, hist)
        return remote(tp.at[to], tb.at[q], tp_s.at[k - 1], tp_r.at[k - 1], to, c)

    def send_coeffs(k, base):
        return remote(cb.at[q - base], cb.at[q - base], cb_s.at[k - 1], cb_r.at[k - 1],
                      base + lax.rem(q - base + k, hist), c)

    relay = remote(cb.at[q], cb.at[q], cb_s.at[hist - 1], cb_r.at[hist - 1], q + hist, c)
    give_count = remote(cnt, cnt, ct_s.at[0], ct_r.at[0], q + hist, c)

    @pl.when(is_hist)
    def _():
        @pl.loop(0, slots)
        def _(s):
            weighted = jnp.where(date < hl_ref[0], ccl[:, cols(s)] * cv[:, cols(s)], 0.0)
            for k in range(COLS):
                tp[s, k : k + 1, :] = jnp.sum(weighted * dm[:, k : k + 1], axis=0, keepdims=True)

        @pl.loop(1, hist)
        def _(k):
            send_target(k).start()

        start_early(third, most)
        ratio_ref[...] = jnp.zeros_like(ratio_ref)
        peak_ref[...] = jnp.zeros_like(peak_ref)
        keep_o.wait()

        @pl.loop(1, 2 * hist)
        def _(k):
            send_words(k).wait_recv()

        start = c * (half // 32) + q * (own // 32)
        flags = clear_bits(ow[...], lax.rem(start, 128), own)
        day = lax.broadcasted_iota(jnp.int32, flags.shape, 0)
        nm[...] = dot_high(ot_ref[...], jnp.where(day < hl_ref[0], flags, 0.0))
        cnt[...] = nm[0:1, :]
        give_count.start()
        total = tp[q]

        @pl.loop(1, hist)
        def _(k):
            send_target(k).wait_recv()

        tb[q] = total
        total = tb[0]
        for s in range(1, hist):
            total = total + tb[s]
        tb[q] = total

        def entry(i, j):
            at = i * (i + 1) // 2 + j
            return nm[at : at + 1, :]

        answer = solve_rows(entry, lambda i: tb[q, i : i + 1, :])
        for i in range(COLS):
            cb[q, i : i + 1, :] = answer[i]
        relay.start()

        @pl.loop(1, hist)
        def _(k):
            send_coeffs(k, 0).start()

        start_early(most, slots)

        @pl.loop(1, hist)
        def _(k):
            send_coeffs(k, 0).wait_recv()

    @pl.when(is_late)
    def _():
        for h in range(2):
            remote(w_ref, hw.at[pl.ds(h * rows, rows), :], hw_s.at[h], hw_r.at[h], q, 1 - c).wait_recv()

        @pl.loop(0, slots)
        def _(s):
            block, offset = word_block(s)
            rt[:, cols(s)] = clear_bits(hw[:, block], offset, own)

        remote(cb.at[q - hist], cb.at[q - hist], cb_s.at[hist - 1], cb_r.at[hist - 1], q - hist, c).wait_recv()

        @pl.loop(1, hist)
        def _(k):
            send_coeffs(k, hist).start()

        start_early(most, slots)

        @pl.loop(1, hist)
        def _(k):
            send_coeffs(k, hist).wait_recv()

    @pl.loop(0, slots)
    def _(s):
        resid = ccl[:, cols(s)] * (cv[:, cols(s)] - fitted(dm[...], cb[s]))
        cv[:, cols(s)] = resid
        tot[0:1, cols(s)] = jnp.sum(resid, axis=0, keepdims=True)
        sq[s] = jnp.sum(jnp.where(date < hl_ref[0], resid * resid, 0.0), axis=0, keepdims=True)

    def send_total(j):
        return remote(tot, tt.at[j - 1], tt_s.at[j - 1], tt_r.at[j - 1], q + j, c)

    for j in range(1, back):
        @pl.when(jnp.logical_and(q + j >= hist, q + j < chips))
        def _():
            send_total(j).start()

    def send_squares(s):
        return remote(sq.at[s], sb.at[q], sq_s.at[s], sq_r.at[q], hist + s, c)

    @pl.when(is_hist)
    def _():
        @pl.loop(0, hist)
        def _(k):
            send_squares(lax.rem(q + k, hist)).start()

    def send_scale(k):
        to = lax.rem(me - 2 * hist + k, 2 * late)
        return remote(sc, scb.at[c, q - hist], sc_s.at[k - 1], sc_r.at[k - 1],
                      hist + lax.div(to, 2), lax.rem(to, 2))

    def send_max(s, k):
        return remote(mrow.at[s], mb.at[q - hist, s], mx_s.at[s * late + k], mx_r.at[s * late + q - hist], hist + k, c)

    def ratio_out(s):
        return remote(rt.at[theirs, cols(s)], rin.at[:, cols(s)], or_s.at[s], or_r.at[s], q, 1 - c)

    def peak_out(s):
        return remote(hv.at[theirs, cols(s)], pin.at[:, cols(s)], op_s.at[s], op_r.at[s], q, 1 - c)

    @pl.when(is_late)
    def _():
        row = lax.broadcasted_iota(jnp.int32, (chip_rows, 128), 0)
        bounds = jnp.zeros((chip_rows, 128), jnp.int32)
        for i in range(chip_rows):
            bounds = jnp.where(row == i, b_ref[q * chip_rows + i], bounds)
        over = 1.0 / (bounds[:, 0:1].astype(jnp.float32) * 0.001)

        @pl.loop(0, slots)
        def _(s):
            for h in range(2):
                remote(v_ref.at[:, half_col(h, s)], hv.at[pl.ds(h * rows, rows), cols(s)],
                       ha_s.at[h * slots + s], ha_r.at[h * slots + s], q, 1 - c).wait_recv()
            early_resid = rt[:, cols(s)] * (hv[:, cols(s)] - fitted(de[...], cb[s]))
            change = cv[:, cols(s)] - early_resid
            rt[:, cols(s)] = scan_rows(change, jnp.add, 0.0) + jnp.sum(early_resid, axis=0, keepdims=True)

        for j in range(1, back):
            send_total(j).wait_recv()

        @pl.loop(0, slots)
        def _(s):
            moving = rt[:, cols(s)]
            for j in range(1, back):
                moving = moving + tt[j - 1, 0:1, cols(s)]
            ratio = jnp.where(date >= ms_ref[0], moving * over, 0.0)
            rt[:, cols(s)] = ratio
            best = scan_rows(jnp.abs(ratio), jnp.maximum, 0.0)
            ccl[:, cols(s)] = best
            mrow[s] = best[chip_rows - 1 :, :]

            @pl.loop(q - hist + 1, late)
            def _(k):
                send_max(s, k).start()

            ratio_out(s).start()

        @pl.loop(0, hist)
        def _(s):
            remote(sq.at[s], sb.at[s], sq_s.at[s], sq_r.at[s], q - hist, c).wait_recv()
        give_count.wait_recv()
        squares = sb[0]
        for s in range(1, hist):
            squares = squares + sb[s]
        count = cnt[...]
        sigma = jnp.sqrt(squares / (count - COLS) + 1e-06)
        scale = 1.0 / (sigma * jnp.sqrt(count))
        sc[...] = scale
        scb[c, q - hist] = scale

        @pl.loop(1, 2 * late)
        def _(k):
            send_scale(k).start()

        @pl.loop(0, slots)
        def _(s):
            def earlier(k, best):
                remote(mrow.at[s], mb.at[k, s], mx_s.at[s * late + k], mx_r.at[s * late + k], q, 1 - c).wait_recv()
                return jnp.maximum(best, mb[k, s])

            before = lax.fori_loop(0, q - hist, earlier, jnp.zeros((1, own), jnp.float32))
            hv[:, cols(s)] = jnp.maximum(ccl[:, cols(s)], before)
            peak_out(s).start()

        @pl.loop(1, 2 * late)
        def _(k):
            send_scale(k).wait_recv()

        @pl.loop(0, slots)
        def _(s):
            scale = scb[c, s]
            ratio_ref[:, half_col(c, s)] = rt[mine, cols(s)] * scale
            peak_ref[:, half_col(c, s)] = hv[mine, cols(s)] * scale

        @pl.loop(0, slots)
        def _(s):
            ratio_out(s).wait_recv()
            peak_out(s).wait_recv()
            scale = scb[1 - c, s]
            ratio_ref[:, half_col(1 - c, s)] = rin[:, cols(s)] * scale
            peak_ref[:, half_col(1 - c, s)] = pin[:, cols(s)] * scale

        @pl.loop(0, slots)
        def _(s):
            ratio_out(s).wait_send()
            peak_out(s).wait_send()

            @pl.loop(q - hist + 1, late)
            def _(k):
                send_max(s, k).wait_send()

        @pl.loop(1, 2 * late)
        def _(k):
            send_scale(k).wait_send()

        @pl.loop(1, hist)
        def _(k):
            send_coeffs(k, hist).wait_send()

    swap_v.wait_send()
    swap_w.wait_send()

    @pl.when(is_hist)
    def _():
        @pl.loop(1, 2 * hist)
        def _(k):
            send_words(k).wait_send()

        @pl.loop(1, hist)
        def _(k):
            send_target(k).wait_send()
            send_coeffs(k, 0).wait_send()

        relay.wait_send()
        give_count.wait_send()

        @pl.loop(0, hist)
        def _(s):
            send_squares(s).wait_send()

    @pl.when(sends_early)
    def _():
        for h in range(2):
            early_words(h).wait_send()

        @pl.loop(0, slots)
        def _(s):
            early(0, s).wait_send()
            early(1, s).wait_send()

    for j in range(1, back):
        @pl.when(jnp.logical_and(q + j >= hist, q + j < chips))
        def _():
            send_total(j).wait_send()


def fused_device(narrow, devices, values, cloud_words, history_len, monitor_start, boundary_table):
    rows, pixels = values.shape
    chips, chip_rows, half = devices // 2, 2 * rows, pixels // 2
    dates = boundary_table.shape[0]
    hist, back = HISTORY_MOST // chip_rows, WINDOW // chip_rows
    own, late = half // hist, chips - hist
    design = host_design(dates)
    lower = [(i, j) for i in range(COLS) for j in range(i + 1)]
    outer = np.zeros((40, HISTORY_MOST), np.float32)
    for at, (i, j) in enumerate(lower):
        outer[at] = design[:HISTORY_MOST, i] * design[:HISTORY_MOST, j]
    by_chip = design.reshape(chips, chip_rows, COLS)
    vmem = pl.BlockSpec(memory_space=pltpu.VMEM)
    hbm = pl.BlockSpec(memory_space=pl.ANY)
    smem = pl.BlockSpec(memory_space=pltpu.SMEM)
    f32, i32, dma = jnp.float32, jnp.int32, pltpu.SemaphoreType.DMA
    scratch = [
        pltpu.VMEM((chip_rows, half), f32),
        pltpu.VMEM((chip_rows, pixels // 32), i32),
        pltpu.VMEM((chip_rows, half), f32),
        pltpu.VMEM((chip_rows, half), f32),
        pltpu.VMEM((chip_rows, pixels // 32), i32),
        pltpu.VMEM((HISTORY_MOST, 128), i32),
        pltpu.VMEM((hist, COLS, own), f32),
        pltpu.VMEM((hist, COLS, own), f32),
        pltpu.VMEM((40, own), f32),
        pltpu.VMEM((hist, COLS, own), f32),
        pltpu.VMEM((1, own), f32),
        pltpu.VMEM((hist, 1, own), f32),
        pltpu.VMEM((hist, 1, own), f32),
        pltpu.VMEM((1, half), f32),
        pltpu.VMEM((max(back - 1, 1), 1, half), f32),
        pltpu.VMEM((1, own), f32),
        pltpu.VMEM((2, late, 1, own), f32),
        pltpu.VMEM((chip_rows, half), f32),
        pltpu.VMEM((hist, 1, own), f32),
        pltpu.VMEM((late, hist, 1, own), f32),
        pltpu.VMEM((rows, half), f32),
        pltpu.VMEM((rows, half), f32),
        pltpu.VMEM((chip_rows, COLS), f32),
        pltpu.VMEM((chip_rows, COLS), f32),
        pltpu.VMEM((40, HISTORY_MOST), f32),
    ]
    for number in (2, 2 * hist, 2, 2 * hist, hist, hist, 1, hist, max(back - 1, 1), 2 * late, hist * late, hist, hist):
        scratch += [dma((number,)), dma((number,))]
    scratch.append(dma((6,)))
    return pl.pallas_call(
        functools.partial(fused_kernel, narrow, chips, hist, back),
        out_shape=[jax.ShapeDtypeStruct((rows, pixels), f32)] * 2,
        in_specs=[smem, smem, smem, vmem, vmem, hbm, hbm],
        out_specs=[vmem, vmem],
        scratch_shapes=scratch,
        compiler_params=pltpu.CompilerParams(has_side_effects=True),
    )(
        history_len, monitor_start, boundary_table, values, cloud_words,
        jnp.asarray(by_chip), jnp.asarray(outer),
    )


def fits(narrow, devices, rows, pixels):
    chip_rows = 2 * rows
    if narrow % 2 or rows % 8 or HISTORY_MOST % chip_rows or WINDOW % chip_rows:
        return False
    hist = HISTORY_MOST // chip_rows
    return devices // 2 == 2 * hist and (pixels // 2) % (hist * 128) == 0 and 128 % (pixels // 64 // hist) == 0


def solution(mesh):
    narrow = mesh.shape["narrow"]
    devices = narrow * mesh.shape["wide"]

    def per_device_any(values, *rest):
        if fits(narrow, devices, *values.shape):
            return fused_device(narrow, devices, values, *rest)
        return per_device(values, *rest)

    placed = (P(("wide", "narrow"), None), P(("wide", "narrow"), None), P(), P(), P())
    return jax.shard_map(
        per_device_any,
        mesh=mesh,
        in_specs=placed,
        out_specs=(P(("wide", "narrow"), None), P(("wide", "narrow"), None)),
        check_vma=False,
    )
```

profile of v0, /device:TPU:17, one launch (start us, length us, event | category | flops | bytes accessed | tf_op | source)
XLA Modules:
  0.0 60.2 jit_solution(1690836045393875904)
XLA Ops:
  1.9 55.0 %shard_map.86 = (f32[16,16384]{1,0:T(8,128)}, f32[16,16384]{1,0:T(8,128)}) custom-call(s32[1]{0:T(128)S(6)} %copy.11.hl_ref, s32[1]{0:T(128)S(6)} %copy.12.ms_ref, s32[512]{0:T(512)} %b_ref.1, f32[16,16384]{1,0:T(8,128)} %v_ref.1, s32[16,512]{1,0:T(8,128)} %w_ref.1, f32[16,32,8]{2,1,0:T(8,128)} %constant.4.clone.d_hbm, f32[40,256]{1,0:T(8,128)} %constant.5.clone.ot_hbm), custom_call_target="tpu_custom_call" | custom-call | tf_op jit(solution)/shard_map/pallas_call | solution.py:618
  56.9 0.0 copy-start
  56.9 2.4 %copy.13 = f32[16,16384]{1,0:T(8,128)} copy(f32[16,16384]{1,0:T(8,128)} %get-tuple-element.4) | data formatting | bytes 2097152
  59.3 0.0 copy-done
  59.3 1.0 %copy.14 = f32[16,16384]{1,0:T(8,128)} copy(f32[16,16384]{1,0:T(8,128)S(1)} %copy-done) | data formatting | bytes 2097152
Async XLA Ops:
  56.9 2.4 %copy-start = (f32[16,16384]{1,0:T(8,128)S(1)}, f32[16,16384]{1,0:T(8,128)}, u32[]{:S(2)}) copy-start(f32[16,16384]{1,0:T(8,128)} %get-tuple-element.5) | copy-start | bytes 3145732
where the time goes:
time: 60.4 us; the launch traced here: 60.2 us
  Pallas kernels  55 us (91%)
  local copies, waits for them, and re-layouts  3.32 us (5%)
  between operations  1.94 us (3%)
    pallas_call x1, Pallas kernels, fused_device(): pl.pallas_call(functools.partial(fused_kernel, narrow, chips, hist, back)...  55 us
    unnamed x4, local copies, waits for them, and re-layouts  3.32 us

commit v1 on v0

--- a/solution.py
+++ b/solution.py
@@ -184,9 +184,9 @@
 
 def fused_kernel(
     narrow, chips, hist, back,
-    hl_ref, ms_ref, b_ref, v_ref, w_ref, d_hbm, ot_hbm, ratio_ref, peak_ref,
-    cv, cw, ccl, hv, hw, ow, tp, tb, nm, cb, cnt, sq, sb, tot, tt, sc, scb, rt, mrow, mb, rin, pin, dm, de, ot_ref,
-    ax_s, ax_r, ha_s, ha_r, hw_s, hw_r, ow_s, ow_r, tp_s, tp_r, cb_s, cb_r, ct_s, ct_r,
+    hl_hbm, ms_hbm, b_hbm, v_hbm, w_hbm, d_hbm, ot_hbm, ratio_ref, peak_ref,
+    hl_ref, ms_ref, b_ref, v_ref, w_ref, cv, cw, ccl, hv, hw, ow, tp, tb, nm, cb, cnt, sq, sb, tot, tt, sc, scb, rt, mrow, mb, dm, de, ot_ref,
+    ax_s, ax_r, ha_s, ha_r, fw_s, hw_s, hw_r, ow_s, ow_r, tp_s, tp_r, cb_s, cb_r, ct_s, ct_r,
     sq_s, sq_r, tt_s, tt_r, sc_s, sc_r, mx_s, mx_r, or_s, or_r, op_s, op_r, lc,
 ):
     me = lax.axis_index("wide") * narrow + lax.axis_index("narrow")
@@ -209,6 +209,9 @@
             src_ref=src, dst_ref=dst, send_sem=ssem, recv_sem=rsem,
             device_id=dev(q2, c2), device_id_type=MESH)
 
+    def drain(ref, sem):
+        pltpu.make_async_copy(ref, ref, sem).wait()
+
     def cols(s):
         return pl.ds(pl.multiple_of(s * own, own), own)
 
@@ -220,20 +223,44 @@
     def half_col(h, s):
         return pl.ds(pl.multiple_of(h * half + s * own, own), own)
 
+    get_w = pltpu.make_async_copy(w_hbm, w_ref, lc.at[6])
+    get_v = pltpu.make_async_copy(v_hbm, v_ref, lc.at[7])
+    keep_v = pltpu.make_async_copy(v_hbm.at[:, my_half], cv.at[mine, :], lc.at[0])
+    keep_w = pltpu.make_async_copy(w_hbm, cw.at[mine, :], lc.at[1])
+    get_scalars = [
+        pltpu.make_async_copy(hl_hbm, hl_ref, lc.at[8]),
+        pltpu.make_async_copy(ms_hbm, ms_ref, lc.at[9]),
+        pltpu.make_async_copy(b_hbm, b_ref, lc.at[10]),
+    ]
+    barrier = pltpu.get_barrier_semaphore()
+    devices = 2 * chips
+
+    @pl.loop(1, devices)
+    def _(k):
+        to = lax.rem(me + k, devices)
+        pl.semaphore_signal(
+            barrier, inc=1, device_id=(lax.div(to, narrow), lax.rem(to, narrow)), device_id_type=MESH)
+
+    get_w.start()
+    get_v.start()
+    keep_w.start()
+    keep_v.start()
+    for get in get_scalars:
+        get.start()
+
     swap_v = remote(v_ref.at[:, other_half], cv.at[mine, :], ax_s.at[0], ax_r.at[0], q, 1 - c)
     swap_w = remote(w_ref, cw.at[mine, :], ax_s.at[1], ax_r.at[1], q, 1 - c)
-    swap_w.start()
-    swap_v.start()
     get_d = pltpu.make_async_copy(d_hbm.at[q], dm, lc.at[3])
     get_e = pltpu.make_async_copy(d_hbm.at[lax.max(q - back, 0)], de, lc.at[4])
     get_o = pltpu.make_async_copy(ot_hbm, ot_ref, lc.at[5])
     get_d.start()
     get_e.start()
     get_o.start()
-    keep_v = pltpu.make_async_copy(v_ref.at[:, my_half], cv.at[mine, :], lc.at[0])
-    keep_w = pltpu.make_async_copy(w_ref, cw.at[mine, :], lc.at[1])
-    keep_v.start()
-    keep_w.start()
+    get_w.wait()
+    get_v.wait()
+    pl.semaphore_wait(barrier, devices - 1)
+    swap_w.start()
+    swap_v.start()
 
     def owner_block(q2, c2):
         return pl.ds(pl.multiple_of(lax.div(c2 * half + q2 * own, 32 * 128) * 128, 128), 128)
@@ -244,7 +271,7 @@
     def send_words(k):
         to = lax.rem(me + k, 2 * hist)
         return remote(w_ref.at[:, owner_block(lax.div(to, 2), lax.rem(to, 2))],
-                      ow.at[my_dates, :], ow_s.at[k - 1], ow_r.at[k - 1],
+                      ow.at[my_dates, :], ow_s.at[0], ow_r.at[0],
                       lax.div(to, 2), lax.rem(to, 2))
 
     @pl.when(is_hist)
@@ -255,34 +282,49 @@
         keep_o.start()
 
     sends_early = jnp.logical_and(q + back >= hist, q + back < chips)
+    splits = jnp.logical_and(q + back >= hist, is_hist)
+    forwards = jnp.logical_and(q + 2 * back >= hist, q + back < hist)
+    direct = slots // 2
+    later = slots * 3 // 4
 
     def early_words(h):
-        return remote(w_ref, hw.at[mine, :], hw_s.at[h], hw_r.at[c], q + back, h)
-
-    def early(h, s):
+        return remote(w_ref, hw.at[mine, :], hw_s.at[0], hw_r.at[0], q + back, h)
+
+    def early(h, s, to):
         return remote(v_ref.at[:, half_col(h, s)], hv.at[mine, cols(s)],
-                      ha_s.at[h * slots + s], ha_r.at[c * slots + s], q + back, h)
-
-    third, most = slots // 4, slots * 5 // 8
-
-    def start_early(low, high):
-        @pl.when(sends_early)
+                      ha_s.at[0], ha_r.at[s], to, h)
+
+    def forward(s):
+        return remote(hv.at[:, cols(s)], hv.at[:, cols(s)], fw_s.at[0], ha_r.at[s], q + 2 * back, c)
+
+    most = slots * 5 // 8
+
+    def start_early(when, low, high, to):
+        @pl.when(when)
         def _():
             @pl.loop(low, high)
             def _(s):
-                early(0, s).start()
-                early(1, s).start()
+                early(0, s, to).start()
+                early(1, s, to).start()
+
+    def pass_on(low, high):
+        @pl.when(forwards)
+        def _():
+            @pl.loop(low, high)
+            def _(s):
+                drain(hv.at[:, cols(s)], ha_r.at[s])
+                forward(s).start()
+
+    late_sends = jnp.logical_and(is_late, sends_early)
 
     @pl.when(sends_early)
     def _():
         for h in range(2):
             early_words(h).start()
 
-    start_early(0, third)
-
-    @pl.when(is_late)
-    def _():
-        start_early(third, most)
+    start_early(splits, direct, later, q - back)
+    start_early(splits, 0, direct, q + back)
+    start_early(late_sends, 0, most, q + back)
 
     def word_block(s):
         start = c * (half // 32) + s * (own // 32)
@@ -302,17 +344,19 @@
     get_d.wait()
     get_e.wait()
     get_o.wait()
+    for get in get_scalars:
+        get.wait()
     date = q * chip_rows + lax.broadcasted_iota(jnp.int32, (chip_rows, own), 0)
 
     def send_target(k):
         to = lax.rem(q + k, hist)
-        return remote(tp.at[to], tb.at[q], tp_s.at[k - 1], tp_r.at[k - 1], to, c)
+        return remote(tp.at[to], tb.at[q], tp_s.at[0], tp_r.at[0], to, c)
 
     def send_coeffs(k, base):
-        return remote(cb.at[q - base], cb.at[q - base], cb_s.at[k - 1], cb_r.at[k - 1],
+        return remote(cb.at[q - base], cb.at[q - base], cb_s.at[0], cb_r.at[0],
                       base + lax.rem(q - base + k, hist), c)
 
-    relay = remote(cb.at[q], cb.at[q], cb_s.at[hist - 1], cb_r.at[hist - 1], q + hist, c)
+    relay = remote(cb.at[q], cb.at[q], cb_s.at[0], cb_r.at[1], q + hist, c)
     give_count = remote(cnt, cnt, ct_s.at[0], ct_r.at[0], q + hist, c)
 
     @pl.when(is_hist)
@@ -327,14 +371,13 @@
         def _(k):
             send_target(k).start()
 
-        start_early(third, most)
+        start_early(splits, later, slots, q - back)
         ratio_ref[...] = jnp.zeros_like(ratio_ref)
         peak_ref[...] = jnp.zeros_like(peak_ref)
         keep_o.wait()
 
-        @pl.loop(1, 2 * hist)
-        def _(k):
-            send_words(k).wait_recv()
+        others = ow.at[pl.ds(0, (2 * hist - 1) * rows), :]
+        drain(others, ow_r.at[0])
 
         start = c * (half // 32) + q * (own // 32)
         flags = clear_bits(ow[...], lax.rem(start, 128), own)
@@ -343,10 +386,8 @@
         cnt[...] = nm[0:1, :]
         give_count.start()
         total = tp[q]
-
-        @pl.loop(1, hist)
-        def _(k):
-            send_target(k).wait_recv()
+        pass_on(direct, later)
+        drain(tb.at[pl.ds(0, hist - 1)], tp_r.at[0])
 
         tb[q] = total
         total = tb[0]
@@ -367,33 +408,26 @@
         def _(k):
             send_coeffs(k, 0).start()
 
-        start_early(most, slots)
-
-        @pl.loop(1, hist)
-        def _(k):
-            send_coeffs(k, 0).wait_recv()
+        pass_on(later, slots)
+        drain(cb.at[pl.ds(0, hist - 1)], cb_r.at[0])
 
     @pl.when(is_late)
     def _():
-        for h in range(2):
-            remote(w_ref, hw.at[pl.ds(h * rows, rows), :], hw_s.at[h], hw_r.at[h], q, 1 - c).wait_recv()
+        drain(hw, hw_r.at[0])
 
         @pl.loop(0, slots)
         def _(s):
             block, offset = word_block(s)
             rt[:, cols(s)] = clear_bits(hw[:, block], offset, own)
 
-        remote(cb.at[q - hist], cb.at[q - hist], cb_s.at[hist - 1], cb_r.at[hist - 1], q - hist, c).wait_recv()
+        remote(cb.at[q - hist], cb.at[q - hist], cb_s.at[0], cb_r.at[1], q - hist, c).wait_recv()
 
         @pl.loop(1, hist)
         def _(k):
             send_coeffs(k, hist).start()
 
-        start_early(most, slots)
-
-        @pl.loop(1, hist)
-        def _(k):
-            send_coeffs(k, hist).wait_recv()
+        start_early(late_sends, most, slots, q + back)
+        drain(cb.at[pl.ds(0, hist - 1)], cb_r.at[0])
 
     @pl.loop(0, slots)
     def _(s):
@@ -411,7 +445,7 @@
             send_total(j).start()
 
     def send_squares(s):
-        return remote(sq.at[s], sb.at[q], sq_s.at[s], sq_r.at[q], hist + s, c)
+        return remote(sq.at[s], sb.at[q], sq_s.at[0], sq_r.at[0], hist + s, c)
 
     @pl.when(is_hist)
     def _():
@@ -420,18 +454,18 @@
             send_squares(lax.rem(q + k, hist)).start()
 
     def send_scale(k):
-        to = lax.rem(me - 2 * hist + k, 2 * late)
-        return remote(sc, scb.at[c, q - hist], sc_s.at[k - 1], sc_r.at[k - 1],
-                      hist + lax.div(to, 2), lax.rem(to, 2))
-
-    def send_max(s, k):
-        return remote(mrow.at[s], mb.at[q - hist, s], mx_s.at[s * late + k], mx_r.at[s * late + q - hist], hist + k, c)
+        return remote(sc, scb.at[q - hist], sc_s.at[0], sc_r.at[0],
+                      hist + lax.rem(q - hist + k, late), c)
+
+    def send_max(group, k):
+        some = pl.ds(group * direct, direct)
+        return remote(mrow.at[some], mb.at[q - hist, some], mx_s.at[k], mx_r.at[q - hist], hist + k, c)
 
     def ratio_out(s):
-        return remote(rt.at[theirs, cols(s)], rin.at[:, cols(s)], or_s.at[s], or_r.at[s], q, 1 - c)
+        return remote(rt.at[theirs, cols(s)], ratio_ref.at[:, half_col(c, s)], or_s.at[0], or_r.at[0], q, 1 - c)
 
     def peak_out(s):
-        return remote(hv.at[theirs, cols(s)], pin.at[:, cols(s)], op_s.at[s], op_r.at[s], q, 1 - c)
+        return remote(hv.at[theirs, cols(s)], peak_ref.at[:, half_col(c, s)], op_s.at[0], op_r.at[0], q, 1 - c)
 
     @pl.when(is_late)
     def _():
@@ -441,38 +475,7 @@
             bounds = jnp.where(row == i, b_ref[q * chip_rows + i], bounds)
         over = 1.0 / (bounds[:, 0:1].astype(jnp.float32) * 0.001)
 
-        @pl.loop(0, slots)
-        def _(s):
-            for h in range(2):
-                remote(v_ref.at[:, half_col(h, s)], hv.at[pl.ds(h * rows, rows), cols(s)],
-                       ha_s.at[h * slots + s], ha_r.at[h * slots + s], q, 1 - c).wait_recv()
-            early_resid = rt[:, cols(s)] * (hv[:, cols(s)] - fitted(de[...], cb[s]))
-            change = cv[:, cols(s)] - early_resid
-            rt[:, cols(s)] = scan_rows(change, jnp.add, 0.0) + jnp.sum(early_resid, axis=0, keepdims=True)
-
-        for j in range(1, back):
-            send_total(j).wait_recv()
-
-        @pl.loop(0, slots)
-        def _(s):
-            moving = rt[:, cols(s)]
-            for j in range(1, back):
-                moving = moving + tt[j - 1, 0:1, cols(s)]
-            ratio = jnp.where(date >= ms_ref[0], moving * over, 0.0)
-            rt[:, cols(s)] = ratio
-            best = scan_rows(jnp.abs(ratio), jnp.maximum, 0.0)
-            ccl[:, cols(s)] = best
-            mrow[s] = best[chip_rows - 1 :, :]
-
-            @pl.loop(q - hist + 1, late)
-            def _(k):
-                send_max(s, k).start()
-
-            ratio_out(s).start()
-
-        @pl.loop(0, hist)
-        def _(s):
-            remote(sq.at[s], sb.at[s], sq_s.at[s], sq_r.at[s], q - hist, c).wait_recv()
+        drain(sb, sq_r.at[0])
         give_count.wait_recv()
         squares = sb[0]
         for s in range(1, hist):
@@ -481,92 +484,104 @@
         sigma = jnp.sqrt(squares / (count - COLS) + 1e-06)
         scale = 1.0 / (sigma * jnp.sqrt(count))
         sc[...] = scale
-        scb[c, q - hist] = scale
-
-        @pl.loop(1, 2 * late)
+        scb[q - hist] = scale
+
+        @pl.loop(1, late)
         def _(k):
             send_scale(k).start()
+
+        for j in range(1, back):
+            send_total(j).wait_recv()
+
+        for group in range(2):
+            @pl.loop(group * direct, (group + 1) * direct)
+            def _(s):
+                drain(hv.at[:, cols(s)], ha_r.at[s])
+                early_resid = rt[:, cols(s)] * (hv[:, cols(s)] - fitted(de[...], cb[s]))
+                change = cv[:, cols(s)] - early_resid
+                moving = scan_rows(change, jnp.add, 0.0) + jnp.sum(early_resid, axis=0, keepdims=True)
+                for j in range(1, back):
+                    moving = moving + tt[j - 1, 0:1, cols(s)]
+                ratio = jnp.where(date >= ms_ref[0], moving * over, 0.0)
+                rt[:, cols(s)] = ratio
+                best = scan_rows(jnp.abs(ratio), jnp.maximum, 0.0)
+                ccl[:, cols(s)] = best
+                mrow[s] = best[chip_rows - 1 :, :]
+
+            @pl.loop(q - hist + 1, late)
+            def _(k):
+                send_max(group, k).start()
+
+        drain(scb.at[pl.ds(0, late - 1)], sc_r.at[0])
+
+        @pl.loop(0, slots)
+        def _(s):
+            scaled = rt[:, cols(s)] * scb[s]
+            rt[:, cols(s)] = scaled
+            ratio_out(s).start()
+            ratio_ref[:, half_col(c, s)] = rt[mine, cols(s)]
+
+        @pl.loop(0, q - hist)
+        def _(k):
+            drain(mrow, mx_r.at[k])
 
         @pl.loop(0, slots)
         def _(s):
             def earlier(k, best):
-                remote(mrow.at[s], mb.at[k, s], mx_s.at[s * late + k], mx_r.at[s * late + k], q, 1 - c).wait_recv()
                 return jnp.maximum(best, mb[k, s])
 
             before = lax.fori_loop(0, q - hist, earlier, jnp.zeros((1, own), jnp.float32))
-            hv[:, cols(s)] = jnp.maximum(ccl[:, cols(s)], before)
+            hv[:, cols(s)] = jnp.maximum(ccl[:, cols(s)], before) * scb[s]
             peak_out(s).start()
-
-        @pl.loop(1, 2 * late)
-        def _(k):
-            send_scale(k).wait_recv()
-
-        @pl.loop(0, slots)
-        def _(s):
-            scale = scb[c, s]
-            ratio_ref[:, half_col(c, s)] = rt[mine, cols(s)] * scale
-            peak_ref[:, half_col(c, s)] = hv[mine, cols(s)] * scale
-
-        @pl.loop(0, slots)
-        def _(s):
-            ratio_out(s).wait_recv()
-            peak_out(s).wait_recv()
-            scale = scb[1 - c, s]
-            ratio_ref[:, half_col(1 - c, s)] = rin[:, cols(s)] * scale
-            peak_ref[:, half_col(1 - c, s)] = pin[:, cols(s)] * scale
-
-        @pl.loop(0, slots)
-        def _(s):
-            ratio_out(s).wait_send()
-            peak_out(s).wait_send()
-
-            @pl.loop(q - hist + 1, late)
-            def _(k):
-                send_max(s, k).wait_send()
-
-        @pl.loop(1, 2 * late)
-        def _(k):
-            send_scale(k).wait_send()
-
-        @pl.loop(1, hist)
-        def _(k):
-            send_coeffs(k, hist).wait_send()
+            peak_ref[:, half_col(c, s)] = hv[mine, cols(s)]
+
+        drain(ratio_ref.at[:, other_half], or_r.at[0])
+        drain(peak_ref.at[:, other_half], op_r.at[0])
+        drain(ratio_ref.at[:, other_half], or_s.at[0])
+        drain(peak_ref.at[:, other_half], op_s.at[0])
+
+        @pl.loop(q - hist + 1, late)
+        def _(k):
+            drain(mrow, mx_s.at[k])
+
+        drain(scb.at[pl.ds(0, late - 1)], sc_s.at[0])
+        drain(cb.at[pl.ds(0, hist - 1)], cb_s.at[0])
 
     swap_v.wait_send()
     swap_w.wait_send()
 
     @pl.when(is_hist)
     def _():
-        @pl.loop(1, 2 * hist)
-        def _(k):
-            send_words(k).wait_send()
-
-        @pl.loop(1, hist)
-        def _(k):
-            send_target(k).wait_send()
-            send_coeffs(k, 0).wait_send()
-
-        relay.wait_send()
+        drain(ow.at[pl.ds(0, (2 * hist - 1) * rows), :], ow_s.at[0])
+        drain(tb.at[pl.ds(0, hist - 1)], tp_s.at[0])
+        drain(cb, cb_s.at[0])
         give_count.wait_send()
-
-        @pl.loop(0, hist)
-        def _(s):
-            send_squares(s).wait_send()
+        drain(sq, sq_s.at[0])
 
     @pl.when(sends_early)
     def _():
-        for h in range(2):
-            early_words(h).wait_send()
-
-        @pl.loop(0, slots)
-        def _(s):
-            early(0, s).wait_send()
-            early(1, s).wait_send()
+        drain(hw, hw_s.at[0])
+        drain(v_ref, ha_s.at[0])
+
+    @pl.when(forwards)
+    def _():
+        drain(hv.at[:, pl.ds(direct * own, half - direct * own)], fw_s.at[0])
 
     for j in range(1, back):
         @pl.when(jnp.logical_and(q + j >= hist, q + j < chips))
         def _():
             send_total(j).wait_send()
+
+
+def store_kernel(ratio_ref, peak_ref, ratio_hbm, peak_hbm, sems):
+    copies = [
+        pltpu.make_async_copy(ratio_ref, ratio_hbm, sems.at[0]),
+        pltpu.make_async_copy(peak_ref, peak_hbm, sems.at[1]),
+    ]
+    for copy in copies:
+        copy.start()
+    for copy in copies:
+        copy.wait()
 
 
 def fused_device(narrow, devices, values, cloud_words, history_len, monitor_start, boundary_table):
@@ -581,11 +596,14 @@
     for at, (i, j) in enumerate(lower):
         outer[at] = design[:HISTORY_MOST, i] * design[:HISTORY_MOST, j]
     by_chip = design.reshape(chips, chip_rows, COLS)
-    vmem = pl.BlockSpec(memory_space=pltpu.VMEM)
-    hbm = pl.BlockSpec(memory_space=pl.ANY)
-    smem = pl.BlockSpec(memory_space=pltpu.SMEM)
+    hbm = pl.BlockSpec(memory_space=pltpu.HBM)
     f32, i32, dma = jnp.float32, jnp.int32, pltpu.SemaphoreType.DMA
     scratch = [
+        pltpu.SMEM((1,), i32),
+        pltpu.SMEM((1,), i32),
+        pltpu.SMEM((dates,), i32),
+        pltpu.VMEM((rows, pixels), f32),
+        pltpu.VMEM((rows, pixels // 32), i32),
         pltpu.VMEM((chip_rows, half), f32),
         pltpu.VMEM((chip_rows, pixels // 32), i32),
         pltpu.VMEM((chip_rows, half), f32),
@@ -602,30 +620,40 @@
         pltpu.VMEM((1, half), f32),
         pltpu.VMEM((max(back - 1, 1), 1, half), f32),
         pltpu.VMEM((1, own), f32),
-        pltpu.VMEM((2, late, 1, own), f32),
+        pltpu.VMEM((late, 1, own), f32),
         pltpu.VMEM((chip_rows, half), f32),
         pltpu.VMEM((hist, 1, own), f32),
         pltpu.VMEM((late, hist, 1, own), f32),
-        pltpu.VMEM((rows, half), f32),
-        pltpu.VMEM((rows, half), f32),
         pltpu.VMEM((chip_rows, COLS), f32),
         pltpu.VMEM((chip_rows, COLS), f32),
         pltpu.VMEM((40, HISTORY_MOST), f32),
     ]
-    for number in (2, 2 * hist, 2, 2 * hist, hist, hist, 1, hist, max(back - 1, 1), 2 * late, hist * late, hist, hist):
+    scratch += [dma((2,)), dma((2,)), dma((1,)), dma((hist,)), dma((1,))]
+    for number in (1, 1, 1):
         scratch += [dma((number,)), dma((number,))]
-    scratch.append(dma((6,)))
-    return pl.pallas_call(
+    scratch += [dma((1,)), dma((2,))]
+    for number in (1, 1, max(back - 1, 1), 1, late, 1, 1):
+        scratch += [dma((number,)), dma((number,))]
+    scratch.append(dma((11,)))
+    outs = pl.pallas_call(
         functools.partial(fused_kernel, narrow, chips, hist, back),
-        out_shape=[jax.ShapeDtypeStruct((rows, pixels), f32)] * 2,
-        in_specs=[smem, smem, smem, vmem, vmem, hbm, hbm],
-        out_specs=[vmem, vmem],
+        out_shape=[pltpu.VMEM((rows, pixels), f32)] * 2,
+        in_specs=[hbm] * 7,
         scratch_shapes=scratch,
-        compiler_params=pltpu.CompilerParams(has_side_effects=True),
+        compiler_params=pltpu.CompilerParams(
+            has_side_effects=True, collective_id=0, vmem_limit_bytes=67043328 - 2 * rows * pixels * 4),
     )(
         history_len, monitor_start, boundary_table, values, cloud_words,
         jnp.asarray(by_chip), jnp.asarray(outer),
     )
+    return pl.pallas_call(
+        store_kernel,
+        out_shape=[jax.ShapeDtypeStruct((rows, pixels), f32)] * 2,
+        in_specs=[pl.BlockSpec(memory_space=pltpu.VMEM)] * 2,
+        out_specs=[pl.BlockSpec(memory_space=pl.ANY)] * 2,
+        scratch_shapes=[dma((2,))],
+        compiler_params=pltpu.CompilerParams(vmem_limit_bytes=8 * 1024 * 1024),
+    )(*outs)
 
 
 def fits(narrow, devices, rows, pixels):

time: 60.4 us -> 45.7 us (0.76)
  the two profiles are of different devices: /device:TPU:17 before, /device:TPU:31 now
where the time goes in v1:
time: 45.7 us; the launch traced here: 45.5 us
  Pallas kernels  43.6 us (95%)
  between operations  1.93 us (4%)
    pallas_call x1, Pallas kernels, fused_device(): pl.pallas_call(functools.partial(fused_kernel, narrow, chips, hist, back)...  42.2 us
    pallas_call x1, Pallas kernels, fused_device(): pl.pallas_call(store_kernel, out_shape=[jax.ShapeDtypeStruct((rows, pixel...  1.33 us

profile of v1, /device:TPU:31, one launch (start us, length us, event | category | flops | bytes accessed | tf_op | source)
XLA Modules:
  0.0 45.5 jit_solution(4630510457243164935)
XLA Ops:
  1.9 42.2 %shard_map.86 = (f32[16,16384]{1,0:T(8,128)S(1)}, f32[16,16384]{1,0:T(8,128)S(1)}) custom-call(s32[1]{0:T(128)S(6)} %copy.9.hl_hbm, s32[1]{0:T(128)S(6)} %copy.10.ms_hbm, s32[512]{0:T(512)} %b_hbm.1, f32[16,16384]{1,0:T(8,128)} %v_hbm.1, s32[16,512]{1,0:T(8,128)} %w_hbm.1, f32[16,32,8]{2,1,0:T(8,128)} %constant.4.clone.d_hbm, f32[40,256]{1,0:T(8,128)} %constant.5.clone.ot_hbm), custom_call_target="tpu_custom_call" | custom-call | tf_op jit(solution)/shard_map/pallas_call | solution.py:638
  44.2 1.3 %shard_map.87 = (f32[16,16384]{1,0:T(8,128)}, f32[16,16384]{1,0:T(8,128)}) custom-call(f32[16,16384]{1,0:T(8,128)S(1)} %get-tuple-element.4.ratio_ref, f32[16,16384]{1,0:T(8,128)S(1)} %get-tuple-element.5.peak_ref), custom_call_target="tpu_custom_call" | custom-call | tf_op jit(solution)/shard_map/pallas_call | solution.py:649

commit v2 on v1

--- a/solution.py
+++ b/solution.py
@@ -185,8 +185,8 @@
 def fused_kernel(
     narrow, chips, hist, back,
     hl_hbm, ms_hbm, b_hbm, v_hbm, w_hbm, d_hbm, ot_hbm, ratio_ref, peak_ref,
-    hl_ref, ms_ref, b_ref, v_ref, w_ref, cv, cw, ccl, hv, hw, ow, tp, tb, nm, cb, cnt, sq, sb, tot, tt, sc, scb, rt, mrow, mb, dm, de, ot_ref,
-    ax_s, ax_r, ha_s, ha_r, fw_s, hw_s, hw_r, ow_s, ow_r, tp_s, tp_r, cb_s, cb_r, ct_s, ct_r,
+    hl_ref, ms_ref, b_ref, v_ref, w_ref, cv, cw, ccl, hv, hw, ow, tp, tb, nm, cb, cnt, sq, sb, tot, te, tt, sc, scb, rt, mrow, mb, dm, de, ot_ref,
+    rdy_s, ax_s, ax_r, ha_s, ha_r, fw_s, hw_s, hw_r, ow_s, ow_r, tp_s, tp_r, cb_s, cb_r, ct_s, ct_r,
     sq_s, sq_r, tt_s, tt_r, sc_s, sc_r, mx_s, mx_r, or_s, or_r, op_s, op_r, lc,
 ):
     me = lax.axis_index("wide") * narrow + lax.axis_index("narrow")
@@ -220,6 +220,9 @@
     my_half = pl.ds(pl.multiple_of(c * half, half), half)
     other_half = pl.ds(pl.multiple_of((1 - c) * half, half), half)
 
+    def word_half(h):
+        return pl.ds(pl.multiple_of(h * (half // 32), half // 32), half // 32)
+
     def half_col(h, s):
         return pl.ds(pl.multiple_of(h * half + s * own, own), own)
 
@@ -233,13 +236,24 @@
         pltpu.make_async_copy(b_hbm, b_ref, lc.at[10]),
     ]
     barrier = pltpu.get_barrier_semaphore()
-    devices = 2 * chips
-
-    @pl.loop(1, devices)
-    def _(k):
-        to = lax.rem(me + k, devices)
+    rdy = rdy_s.at[0]
+
+    def greet(to, sem):
         pl.semaphore_signal(
-            barrier, inc=1, device_id=(lax.div(to, narrow), lax.rem(to, narrow)), device_id_type=MESH)
+            sem, inc=1, device_id=(lax.div(to, narrow), lax.rem(to, narrow)), device_id_type=MESH)
+
+    @pl.when(is_hist)
+    def _():
+        @pl.loop(1, 2 * hist)
+        def _(k):
+            greet(lax.rem(me + k, 2 * hist), barrier)
+        greet(me + 2 * hist, barrier)
+
+    @pl.when(is_late)
+    def _():
+        greet(2 * q + 1 - c, barrier)
+        greet(2 * (q - back), barrier)
+        greet(2 * (q - back) + 1, barrier)
 
     get_w.start()
     get_v.start()
@@ -249,7 +263,8 @@
         get.start()
 
     swap_v = remote(v_ref.at[:, other_half], cv.at[mine, :], ax_s.at[0], ax_r.at[0], q, 1 - c)
-    swap_w = remote(w_ref, cw.at[mine, :], ax_s.at[1], ax_r.at[1], q, 1 - c)
+    swap_w = remote(w_ref.at[:, word_half(1 - c)], cw.at[mine, word_half(1 - c)], ax_s.at[1], ax_r.at[1], q, 1 - c)
+    came_w = remote(w_ref.at[:, word_half(c)], cw.at[theirs, word_half(c)], ax_s.at[1], ax_r.at[1], q, 1 - c)
     get_d = pltpu.make_async_copy(d_hbm.at[q], dm, lc.at[3])
     get_e = pltpu.make_async_copy(d_hbm.at[lax.max(q - back, 0)], de, lc.at[4])
     get_o = pltpu.make_async_copy(ot_hbm, ot_ref, lc.at[5])
@@ -258,7 +273,13 @@
     get_o.start()
     get_w.wait()
     get_v.wait()
-    pl.semaphore_wait(barrier, devices - 1)
+    feeds = jnp.logical_and(q + back >= hist, q + back < chips)
+    pl.semaphore_wait(barrier, jnp.where(is_hist, 2 * hist - 1, 2) + jnp.where(feeds, 2, 0))
+
+    @pl.when(is_late)
+    def _():
+        greet(me - 2 * hist, rdy)
+
     swap_w.start()
     swap_v.start()
 
@@ -285,10 +306,11 @@
     splits = jnp.logical_and(q + back >= hist, is_hist)
     forwards = jnp.logical_and(q + 2 * back >= hist, q + back < hist)
     direct = slots // 2
-    later = slots * 3 // 4
+    later = slots - 1
 
     def early_words(h):
-        return remote(w_ref, hw.at[mine, :], hw_s.at[0], hw_r.at[0], q + back, h)
+        some = word_half(h)
+        return remote(w_ref.at[:, some], hw.at[mine, some], hw_s.at[0], hw_r.at[0], q + back, h)
 
     def early(h, s, to):
         return remote(v_ref.at[:, half_col(h, s)], hv.at[mine, cols(s)],
@@ -322,7 +344,6 @@
         for h in range(2):
             early_words(h).start()
 
-    start_early(splits, direct, later, q - back)
     start_early(splits, 0, direct, q + back)
     start_early(late_sends, 0, most, q + back)
 
@@ -332,24 +353,22 @@
         return pl.ds(pl.multiple_of(base, 128), 128), start - base
 
     keep_w.wait()
-    swap_w.wait_recv()
-
-    @pl.loop(0, slots)
-    def _(s):
-        block, offset = word_block(s)
-        ccl[:, cols(s)] = clear_bits(cw[:, block], offset, own)
-
-    keep_v.wait()
-    swap_v.wait_recv()
+    came_w.wait_recv()
+
     get_d.wait()
     get_e.wait()
     get_o.wait()
     for get in get_scalars:
         get.wait()
+    keep_v.wait()
+    swap_v.wait_recv()
     date = q * chip_rows + lax.broadcasted_iota(jnp.int32, (chip_rows, own), 0)
 
-    def send_target(k):
-        to = lax.rem(q + k, hist)
+    def unpack(s):
+        block, offset = word_block(s)
+        ccl[:, cols(s)] = clear_bits(cw[:, block], offset, own)
+
+    def send_target(to):
         return remote(tp.at[to], tb.at[q], tp_s.at[0], tp_r.at[0], to, c)
 
     def send_coeffs(k, base):
@@ -361,17 +380,27 @@
 
     @pl.when(is_hist)
     def _():
-        @pl.loop(0, slots)
-        def _(s):
+        def part(s):
+            unpack(s)
             weighted = jnp.where(date < hl_ref[0], ccl[:, cols(s)] * cv[:, cols(s)], 0.0)
             for k in range(COLS):
                 tp[s, k : k + 1, :] = jnp.sum(weighted * dm[:, k : k + 1], axis=0, keepdims=True)
 
-        @pl.loop(1, hist)
-        def _(k):
-            send_target(k).start()
-
-        start_early(splits, later, slots, q - back)
+        part(lax.rem(q + 1, hist))
+        part(lax.rem(q + 2, hist))
+        pl.semaphore_wait(rdy, 1)
+        send_target(lax.rem(q + 1, hist)).start()
+        send_target(lax.rem(q + 2, hist)).start()
+
+        @pl.loop(3, hist)
+        def _(k):
+            to = lax.rem(q + k, hist)
+            part(to)
+            send_target(to).start()
+
+        part(q)
+
+        start_early(splits, direct, later, q - back)
         ratio_ref[...] = jnp.zeros_like(ratio_ref)
         peak_ref[...] = jnp.zeros_like(peak_ref)
         keep_o.wait()
@@ -386,7 +415,6 @@
         cnt[...] = nm[0:1, :]
         give_count.start()
         total = tp[q]
-        pass_on(direct, later)
         drain(tb.at[pl.ds(0, hist - 1)], tp_r.at[0])
 
         tb[q] = total
@@ -408,12 +436,14 @@
         def _(k):
             send_coeffs(k, 0).start()
 
-        pass_on(later, slots)
+        start_early(splits, later, slots, q + back)
+        pass_on(direct, later)
         drain(cb.at[pl.ds(0, hist - 1)], cb_r.at[0])
 
     @pl.when(is_late)
     def _():
-        drain(hw, hw_r.at[0])
+        pl.loop(0, slots)(unpack)
+        drain(hw.at[:, word_half(c)], hw_r.at[0])
 
         @pl.loop(0, slots)
         def _(s):
@@ -436,13 +466,19 @@
         tot[0:1, cols(s)] = jnp.sum(resid, axis=0, keepdims=True)
         sq[s] = jnp.sum(jnp.where(date < hl_ref[0], resid * resid, 0.0), axis=0, keepdims=True)
 
-    def send_total(j):
-        return remote(tot, tt.at[j - 1], tt_s.at[j - 1], tt_r.at[j - 1], q + j, c)
-
-    for j in range(1, back):
-        @pl.when(jnp.logical_and(q + j >= hist, q + j < chips))
-        def _():
-            send_total(j).start()
+    even = lax.rem(q, 2) == 0
+
+    def group_cols(group):
+        return pl.ds(group * direct * own, direct * own)
+
+    def send_total(group, source, to):
+        some = group_cols(group)
+        return remote(source.at[:, some], tt.at[:, some], tt_s.at[0], tt_r.at[group], to, c)
+
+    @pl.when(jnp.logical_and(is_late, even))
+    def _():
+        for group in range(2):
+            send_total(group, tot, q + 1).start()
 
     def send_squares(s):
         return remote(sq.at[s], sb.at[q], sq_s.at[0], sq_r.at[0], hist + s, c)
@@ -474,6 +510,20 @@
         for i in range(chip_rows):
             bounds = jnp.where(row == i, b_ref[q * chip_rows + i], bounds)
         over = 1.0 / (bounds[:, 0:1].astype(jnp.float32) * 0.001)
+
+        for group in range(2):
+            @pl.loop(group * direct, (group + 1) * direct)
+            def _(s):
+                drain(hv.at[:, cols(s)], ha_r.at[s])
+                early_resid = rt[:, cols(s)] * (hv[:, cols(s)] - fitted(de[...], cb[s]))
+                change = cv[:, cols(s)] - early_resid
+                early_total = jnp.sum(early_resid, axis=0, keepdims=True)
+                te[0:1, cols(s)] = early_total
+                rt[:, cols(s)] = scan_rows(change, jnp.add, 0.0) + early_total
+
+            @pl.when(jnp.logical_not(even))
+            def _():
+                send_total(group, te, q - 1).start()
 
         drain(sb, sq_r.at[0])
         give_count.wait_recv()
@@ -490,18 +540,12 @@
         def _(k):
             send_scale(k).start()
 
-        for j in range(1, back):
-            send_total(j).wait_recv()
-
         for group in range(2):
+            drain(tt.at[:, group_cols(group)], tt_r.at[group])
+
             @pl.loop(group * direct, (group + 1) * direct)
             def _(s):
-                drain(hv.at[:, cols(s)], ha_r.at[s])
-                early_resid = rt[:, cols(s)] * (hv[:, cols(s)] - fitted(de[...], cb[s]))
-                change = cv[:, cols(s)] - early_resid
-                moving = scan_rows(change, jnp.add, 0.0) + jnp.sum(early_resid, axis=0, keepdims=True)
-                for j in range(1, back):
-                    moving = moving + tt[j - 1, 0:1, cols(s)]
+                moving = rt[:, cols(s)] + tt[0:1, cols(s)]
                 ratio = jnp.where(date >= ms_ref[0], moving * over, 0.0)
                 rt[:, cols(s)] = ratio
                 best = scan_rows(jnp.abs(ratio), jnp.maximum, 0.0)
@@ -544,6 +588,7 @@
         def _(k):
             drain(mrow, mx_s.at[k])
 
+        drain(tot, tt_s.at[0])
         drain(scb.at[pl.ds(0, late - 1)], sc_s.at[0])
         drain(cb.at[pl.ds(0, hist - 1)], cb_s.at[0])
 
@@ -560,17 +605,12 @@
 
     @pl.when(sends_early)
     def _():
-        drain(hw, hw_s.at[0])
+        drain(w_ref, hw_s.at[0])
         drain(v_ref, ha_s.at[0])
 
     @pl.when(forwards)
     def _():
-        drain(hv.at[:, pl.ds(direct * own, half - direct * own)], fw_s.at[0])
-
-    for j in range(1, back):
-        @pl.when(jnp.logical_and(q + j >= hist, q + j < chips))
-        def _():
-            send_total(j).wait_send()
+        drain(hv.at[:, pl.ds(direct * own, (later - direct) * own)], fw_s.at[0])
 
 
 def store_kernel(ratio_ref, peak_ref, ratio_hbm, peak_hbm, sems):
@@ -618,7 +658,8 @@
         pltpu.VMEM((hist, 1, own), f32),
         pltpu.VMEM((hist, 1, own), f32),
         pltpu.VMEM((1, half), f32),
-        pltpu.VMEM((max(back - 1, 1), 1, half), f32),
+        pltpu.VMEM((1, half), f32),
+        pltpu.VMEM((1, half), f32),
         pltpu.VMEM((1, own), f32),
         pltpu.VMEM((late, 1, own), f32),
         pltpu.VMEM((chip_rows, half), f32),
@@ -628,11 +669,15 @@
         pltpu.VMEM((chip_rows, COLS), f32),
         pltpu.VMEM((40, HISTORY_MOST), f32),
     ]
+    scratch += [pltpu.SemaphoreType.REGULAR((1,))]
     scratch += [dma((2,)), dma((2,)), dma((1,)), dma((hist,)), dma((1,))]
     for number in (1, 1, 1):
         scratch += [dma((number,)), dma((number,))]
     scratch += [dma((1,)), dma((2,))]
-    for number in (1, 1, max(back - 1, 1), 1, late, 1, 1):
+    for number in (1, 1):
+        scratch += [dma((number,)), dma((number,))]
+    scratch += [dma((1,)), dma((2,))]
+    for number in (1, late, 1, 1):
         scratch += [dma((number,)), dma((number,))]
     scratch.append(dma((11,)))
     outs = pl.pallas_call(
@@ -658,7 +703,7 @@
 
 def fits(narrow, devices, rows, pixels):
     chip_rows = 2 * rows
-    if narrow % 2 or rows % 8 or HISTORY_MOST % chip_rows or WINDOW % chip_rows:
+    if narrow % 2 or rows % 8 or HISTORY_MOST % chip_rows or WINDOW != 2 * chip_rows:
         return False
     hist = HISTORY_MOST // chip_rows
     return devices // 2 == 2 * hist and (pixels // 2) % (hist * 128) == 0 and 128 % (pixels // 64 // hist) == 0

time: 45.7 us -> 42.9 us (0.939)
  Pallas kernels: 43.6 us -> 40.9 us
    pallas_call x1, Pallas kernels: 42.2 us -> 39.5 us  [fused_device(): pl.pallas_call(functools.partial(fused_kernel, narrow, chips, hist, back)...]
where the time goes in v2:
time: 42.9 us; the launch traced here: 42.8 us
  Pallas kernels  40.9 us (95%)
  between operations  1.93 us (4%)
    pallas_call x1, Pallas kernels, fused_device(): pl.pallas_call(functools.partial(fused_kernel, narrow, chips, hist, back)...  39.5 us
    pallas_call x1, Pallas kernels, fused_device(): pl.pallas_call(store_kernel, out_shape=[jax.ShapeDtypeStruct((rows, pixel...  1.33 us

profile of v2, /device:TPU:31, one launch (start us, length us, event | category | flops | bytes accessed | tf_op | source)
XLA Modules:
  0.0 42.8 jit_solution(4063979736023050966)
XLA Ops:
  1.9 39.5 %shard_map.86 = (f32[16,16384]{1,0:T(8,128)S(1)}, f32[16,16384]{1,0:T(8,128)S(1)}) custom-call(s32[1]{0:T(128)S(6)} %copy.9.hl_hbm, s32[1]{0:T(128)S(6)} %copy.10.ms_hbm, s32[512]{0:T(512)} %b_hbm.1, f32[16,16384]{1,0:T(8,128)} %v_hbm.1, s32[16,512]{1,0:T(8,128)} %w_hbm.1, f32[16,32,8]{2,1,0:T(8,128)} %constant.4.clone.d_hbm, f32[40,256]{1,0:T(8,128)} %constant.5.clone.ot_hbm), custom_call_target="tpu_custom_call" | custom-call | tf_op jit(solution)/shard_map/pallas_call | solution.py:683
  41.4 1.3 %shard_map.87 = (f32[16,16384]{1,0:T(8,128)}, f32[16,16384]{1,0:T(8,128)}) custom-call(f32[16,16384]{1,0:T(8,128)S(1)} %get-tuple-element.4.ratio_ref, f32[16,16384]{1,0:T(8,128)S(1)} %get-tuple-element.5.peak_ref), custom_call_target="tpu_custom_call" | custom-call | tf_op jit(solution)/shard_map/pallas_call | solution.py:694

commit v3 on v2

--- a/solution.py
+++ b/solution.py
@@ -185,8 +185,8 @@
 def fused_kernel(
     narrow, chips, hist, back,
     hl_hbm, ms_hbm, b_hbm, v_hbm, w_hbm, d_hbm, ot_hbm, ratio_ref, peak_ref,
-    hl_ref, ms_ref, b_ref, v_ref, w_ref, cv, cw, ccl, hv, hw, ow, tp, tb, nm, cb, cnt, sq, sb, tot, te, tt, sc, scb, rt, mrow, mb, dm, de, ot_ref,
-    rdy_s, ax_s, ax_r, ha_s, ha_r, fw_s, hw_s, hw_r, ow_s, ow_r, tp_s, tp_r, cb_s, cb_r, ct_s, ct_r,
+    hl_ref, ms_ref, b_ref, v_ref, w_ref, fw, cv, cw, ccl, hv, hw, ow, tp, tb, nm, cb, cnt, sq, sb, tot, tt, sc, scb, rt, mrow, mb, dm, de, ot_ref,
+    rdy_s, ax_s, ax_r, ha_s, ha_r, fw_s, fw_r, hw_s, hw_r, ow_s, ow_r, tp_s, tp_r, cb_s, cb_r, ct_s, ct_r,
     sq_s, sq_r, tt_s, tt_r, sc_s, sc_r, mx_s, mx_r, or_s, or_r, op_s, op_r, lc,
 ):
     me = lax.axis_index("wide") * narrow + lax.axis_index("narrow")
@@ -255,6 +255,14 @@
         greet(2 * (q - back), barrier)
         greet(2 * (q - back) + 1, barrier)
 
+    late_splits = jnp.logical_and(q >= hist + back, q < hist + 2 * back)
+    late_passes = jnp.logical_and(q >= hist, q < hist + back)
+
+    @pl.when(late_passes)
+    def _():
+        greet(2 * (q + back), barrier)
+        greet(2 * (q + back) + 1, barrier)
+
     get_w.start()
     get_v.start()
     keep_w.start()
@@ -274,7 +282,8 @@
     get_w.wait()
     get_v.wait()
     feeds = jnp.logical_and(q + back >= hist, q + back < chips)
-    pl.semaphore_wait(barrier, jnp.where(is_hist, 2 * hist - 1, 2) + jnp.where(feeds, 2, 0))
+    greeted = jnp.where(is_hist, 2 * hist - 1, 2) + jnp.where(feeds, 2, 0) + jnp.where(late_splits, 2, 0)
+    pl.semaphore_wait(barrier, greeted)
 
     @pl.when(is_late)
     def _():
@@ -305,8 +314,9 @@
     sends_early = jnp.logical_and(q + back >= hist, q + back < chips)
     splits = jnp.logical_and(q + back >= hist, is_hist)
     forwards = jnp.logical_and(q + 2 * back >= hist, q + back < hist)
-    direct = slots // 2
+    direct = slots * 3 // 8
     later = slots - 1
+    middle = (direct + later) // 2
 
     def early_words(h):
         some = word_half(h)
@@ -319,7 +329,8 @@
     def forward(s):
         return remote(hv.at[:, cols(s)], hv.at[:, cols(s)], fw_s.at[0], ha_r.at[s], q + 2 * back, c)
 
-    most = slots * 5 // 8
+    most = slots // 2
+    first = slots * 3 // 4
 
     def start_early(when, low, high, to):
         @pl.when(when)
@@ -338,6 +349,17 @@
                 forward(s).start()
 
     late_sends = jnp.logical_and(is_late, sends_early)
+    late_direct = jnp.logical_and(late_sends, jnp.logical_not(late_splits))
+    via = 1
+
+    def early_via(h, i):
+        return remote(v_ref.at[:, half_col(h, most + i)], fw.at[mine, cols(i)], ha_s.at[0], fw_r.at[i], q - back, h)
+
+    def late_forward(i):
+        @pl.when(late_passes)
+        def _():
+            drain(fw.at[:, cols(i)], fw_r.at[i])
+            remote(fw.at[:, cols(i)], hv.at[:, cols(most + i)], fw_s.at[0], ha_r.at[most + i], q + 2 * back, c).start()
 
     @pl.when(sends_early)
     def _():
@@ -371,9 +393,17 @@
     def send_target(to):
         return remote(tp.at[to], tb.at[q], tp_s.at[0], tp_r.at[0], to, c)
 
-    def send_coeffs(k, base):
-        return remote(cb.at[q - base], cb.at[q - base], cb_s.at[0], cb_r.at[0],
-                      base + lax.rem(q - base + k, hist), c)
+    columns = late // 2
+
+    def send_coeffs(k):
+        return remote(cb.at[q], cb.at[q], cb_s.at[0], cb_r.at[0], lax.rem(q + k, hist), c)
+
+    def column_coeffs(k):
+        return remote(cb.at[q - hist], cb.at[q - hist], cb_s.at[0], cb_r.at[1 + k],
+                      hist + lax.rem(q - hist + 2 * k, late), c)
+
+    def cross_coeffs(s):
+        return remote(cb.at[s], cb.at[s], cb_s.at[0], cb_r.at[0], q + 1 - 2 * lax.rem(q, 2), c)
 
     relay = remote(cb.at[q], cb.at[q], cb_s.at[0], cb_r.at[1], q + hist, c)
     give_count = remote(cnt, cnt, ct_s.at[0], ct_r.at[0], q + hist, c)
@@ -400,7 +430,7 @@
 
         part(q)
 
-        start_early(splits, direct, later, q - back)
+        start_early(splits, direct, middle, q - back)
         ratio_ref[...] = jnp.zeros_like(ratio_ref)
         peak_ref[...] = jnp.zeros_like(peak_ref)
         keep_o.wait()
@@ -434,10 +464,11 @@
 
         @pl.loop(1, hist)
         def _(k):
-            send_coeffs(k, 0).start()
-
+            send_coeffs(k).start()
+
+        start_early(splits, middle, later, q - back)
         start_early(splits, later, slots, q + back)
-        pass_on(direct, later)
+        pass_on(direct, middle)
         drain(cb.at[pl.ds(0, hist - 1)], cb_r.at[0])
 
     @pl.when(is_late)
@@ -452,12 +483,28 @@
 
         remote(cb.at[q - hist], cb.at[q - hist], cb_s.at[0], cb_r.at[1], q - hist, c).wait_recv()
 
-        @pl.loop(1, hist)
-        def _(k):
-            send_coeffs(k, hist).start()
-
-        start_early(late_sends, most, slots, q + back)
-        drain(cb.at[pl.ds(0, hist - 1)], cb_r.at[0])
+        @pl.loop(1, columns)
+        def _(k):
+            column_coeffs(k).start()
+
+        cross_coeffs(q - hist).start()
+        start_early(late_direct, most, most + via, q + back)
+        start_early(late_sends, most + via, slots - 1, q + back)
+
+        @pl.when(late_splits)
+        def _():
+            for i in range(via):
+                for h in range(2):
+                    early_via(h, i).start()
+
+        @pl.loop(1, columns)
+        def _(k):
+            from_column = lax.rem(q - hist + late - 2 * k, late)
+            drain(cb.at[from_column], cb_r.at[1 + k])
+            cross_coeffs(from_column).start()
+
+        late_forward(0)
+        drain(cb.at[pl.ds(0, columns)], cb_r.at[0])
 
     @pl.loop(0, slots)
     def _(s):
@@ -466,19 +513,14 @@
         tot[0:1, cols(s)] = jnp.sum(resid, axis=0, keepdims=True)
         sq[s] = jnp.sum(jnp.where(date < hl_ref[0], resid * resid, 0.0), axis=0, keepdims=True)
 
-    even = lax.rem(q, 2) == 0
-
-    def group_cols(group):
-        return pl.ds(group * direct * own, direct * own)
-
-    def send_total(group, source, to):
-        some = group_cols(group)
-        return remote(source.at[:, some], tt.at[:, some], tt_s.at[0], tt_r.at[group], to, c)
-
-    @pl.when(jnp.logical_and(is_late, even))
-    def _():
-        for group in range(2):
-            send_total(group, tot, q + 1).start()
+    totals = jnp.logical_and(q + 1 >= hist, q + 1 < chips)
+    send_total = remote(tot, tt, tt_s.at[0], tt_r.at[0], q + 1, c)
+
+    @pl.when(totals)
+    def _():
+        send_total.start()
+
+    start_early(late_sends, slots - 1, slots, q + back)
 
     def send_squares(s):
         return remote(sq.at[s], sb.at[q], sq_s.at[0], sq_r.at[0], hist + s, c)
@@ -488,13 +530,15 @@
         @pl.loop(0, hist)
         def _(k):
             send_squares(lax.rem(q + k, hist)).start()
+
+        pass_on(middle, later)
 
     def send_scale(k):
         return remote(sc, scb.at[q - hist], sc_s.at[0], sc_r.at[0],
                       hist + lax.rem(q - hist + k, late), c)
 
     def send_max(group, k):
-        some = pl.ds(group * direct, direct)
+        some = pl.ds(0, first) if group == 0 else pl.ds(first, slots - first)
         return remote(mrow.at[some], mb.at[q - hist, some], mx_s.at[k], mx_r.at[q - hist], hist + k, c)
 
     def ratio_out(s):
@@ -511,19 +555,28 @@
             bounds = jnp.where(row == i, b_ref[q * chip_rows + i], bounds)
         over = 1.0 / (bounds[:, 0:1].astype(jnp.float32) * 0.001)
 
-        for group in range(2):
-            @pl.loop(group * direct, (group + 1) * direct)
-            def _(s):
-                drain(hv.at[:, cols(s)], ha_r.at[s])
-                early_resid = rt[:, cols(s)] * (hv[:, cols(s)] - fitted(de[...], cb[s]))
-                change = cv[:, cols(s)] - early_resid
-                early_total = jnp.sum(early_resid, axis=0, keepdims=True)
-                te[0:1, cols(s)] = early_total
-                rt[:, cols(s)] = scan_rows(change, jnp.add, 0.0) + early_total
-
-            @pl.when(jnp.logical_not(even))
-            def _():
-                send_total(group, te, q - 1).start()
+        def window(s):
+            drain(hv.at[:, cols(s)], ha_r.at[s])
+            early_resid = rt[:, cols(s)] * (hv[:, cols(s)] - fitted(de[...], cb[s]))
+            change = cv[:, cols(s)] - early_resid
+            return scan_rows(change, jnp.add, 0.0) + jnp.sum(early_resid, axis=0, keepdims=True)
+
+        def statistic(s, partial):
+            moving = partial + tt[0:1, cols(s)]
+            ratio = jnp.where(date >= ms_ref[0], moving * over, 0.0)
+            rt[:, cols(s)] = ratio
+            best = scan_rows(jnp.abs(ratio), jnp.maximum, 0.0)
+            ccl[:, cols(s)] = best
+            mrow[s] = best[chip_rows - 1 :, :]
+
+        def send_maxima(group):
+            @pl.loop(q - hist + 1, late)
+            def _(k):
+                send_max(group, k).start()
+
+        @pl.loop(0, first)
+        def _(s):
+            rt[:, cols(s)] = window(s)
 
         drain(sb, sq_r.at[0])
         give_count.wait_recv()
@@ -540,22 +593,19 @@
         def _(k):
             send_scale(k).start()
 
-        for group in range(2):
-            drain(tt.at[:, group_cols(group)], tt_r.at[group])
-
-            @pl.loop(group * direct, (group + 1) * direct)
-            def _(s):
-                moving = rt[:, cols(s)] + tt[0:1, cols(s)]
-                ratio = jnp.where(date >= ms_ref[0], moving * over, 0.0)
-                rt[:, cols(s)] = ratio
-                best = scan_rows(jnp.abs(ratio), jnp.maximum, 0.0)
-                ccl[:, cols(s)] = best
-                mrow[s] = best[chip_rows - 1 :, :]
-
-            @pl.loop(q - hist + 1, late)
-            def _(k):
-                send_max(group, k).start()
-
+        send_total.wait_recv()
+
+        @pl.loop(0, first)
+        def _(s):
+            statistic(s, rt[:, cols(s)])
+
+        send_maxima(0)
+
+        @pl.loop(first, slots)
+        def _(s):
+            statistic(s, window(s))
+
+        send_maxima(1)
         drain(scb.at[pl.ds(0, late - 1)], sc_r.at[0])
 
         @pl.loop(0, slots)
@@ -588,7 +638,6 @@
         def _(k):
             drain(mrow, mx_s.at[k])
 
-        drain(tot, tt_s.at[0])
         drain(scb.at[pl.ds(0, late - 1)], sc_s.at[0])
         drain(cb.at[pl.ds(0, hist - 1)], cb_s.at[0])
 
@@ -603,10 +652,18 @@
         give_count.wait_send()
         drain(sq, sq_s.at[0])
 
+    @pl.when(totals)
+    def _():
+        send_total.wait_send()
+
     @pl.when(sends_early)
     def _():
         drain(w_ref, hw_s.at[0])
         drain(v_ref, ha_s.at[0])
+
+    @pl.when(late_passes)
+    def _():
+        drain(fw, fw_s.at[0])
 
     @pl.when(forwards)
     def _():
@@ -644,6 +701,7 @@
         pltpu.SMEM((dates,), i32),
         pltpu.VMEM((rows, pixels), f32),
         pltpu.VMEM((rows, pixels // 32), i32),
+        pltpu.VMEM((chip_rows, own), f32),
         pltpu.VMEM((chip_rows, half), f32),
         pltpu.VMEM((chip_rows, pixels // 32), i32),
         pltpu.VMEM((chip_rows, half), f32),
@@ -659,7 +717,6 @@
         pltpu.VMEM((hist, 1, own), f32),
         pltpu.VMEM((1, half), f32),
         pltpu.VMEM((1, half), f32),
-        pltpu.VMEM((1, half), f32),
         pltpu.VMEM((1, own), f32),
         pltpu.VMEM((late, 1, own), f32),
         pltpu.VMEM((chip_rows, half), f32),
@@ -670,13 +727,13 @@
         pltpu.VMEM((40, HISTORY_MOST), f32),
     ]
     scratch += [pltpu.SemaphoreType.REGULAR((1,))]
-    scratch += [dma((2,)), dma((2,)), dma((1,)), dma((hist,)), dma((1,))]
+    scratch += [dma((2,)), dma((2,)), dma((1,)), dma((hist,)), dma((1,)), dma((1,))]
     for number in (1, 1, 1):
         scratch += [dma((number,)), dma((number,))]
-    scratch += [dma((1,)), dma((2,))]
+    scratch += [dma((1,)), dma((1 + late // 2,))]
     for number in (1, 1):
         scratch += [dma((number,)), dma((number,))]
-    scratch += [dma((1,)), dma((2,))]
+    scratch += [dma((1,)), dma((1,))]
     for number in (1, late, 1, 1):
         scratch += [dma((number,)), dma((number,))]
     scratch.append(dma((11,)))

time: 42.9 us -> 38.6 us (0.90)
  Pallas kernels: 40.9 us -> 36.5 us
    pallas_call x1, Pallas kernels: 39.5 us -> 35.2 us  [fused_device(): pl.pallas_call(functools.partial(fused_kernel, narrow, chips, hist, back)...]
where the time goes in v3:
time: 38.6 us; the launch traced here: 38.5 us
  Pallas kernels  36.5 us (95%)
  between operations  1.93 us (5%)
    pallas_call x1, Pallas kernels, fused_device(): pl.pallas_call(functools.partial(fused_kernel, narrow, chips, hist, back)...  35.2 us
    pallas_call x1, Pallas kernels, fused_device(): pl.pallas_call(store_kernel, out_shape=[jax.ShapeDtypeStruct((rows, pixel...  1.33 us

profile of v3, /device:TPU:31, one launch (start us, length us, event | category | flops | bytes accessed | tf_op | source)
XLA Modules:
  0.0 38.5 jit_solution(15297698154325840743)
XLA Ops:
  1.9 35.2 %shard_map.86 = (f32[16,16384]{1,0:T(8,128)S(1)}, f32[16,16384]{1,0:T(8,128)S(1)}) custom-call(s32[1]{0:T(128)S(6)} %copy.9.hl_hbm, s32[1]{0:T(128)S(6)} %copy.10.ms_hbm, s32[512]{0:T(512)} %b_hbm.1, f32[16,16384]{1,0:T(8,128)} %v_hbm.1, s32[16,512]{1,0:T(8,128)} %w_hbm.1, f32[16,32,8]{2,1,0:T(8,128)} %constant.4.clone.d_hbm, f32[40,256]{1,0:T(8,128)} %constant.5.clone.ot_hbm), custom_call_target="tpu_custom_call" | custom-call | tf_op jit(solution)/shard_map/pallas_call | solution.py:740
  37.1 1.3 %shard_map.87 = (f32[16,16384]{1,0:T(8,128)}, f32[16,16384]{1,0:T(8,128)}) custom-call(f32[16,16384]{1,0:T(8,128)S(1)} %get-tuple-element.4.ratio_ref, f32[16,16384]{1,0:T(8,128)S(1)} %get-tuple-element.5.peak_ref), custom_call_target="tpu_custom_call" | custom-call | tf_op jit(solution)/shard_map/pallas_call | solution.py:751

commit v4 on v3

--- a/solution.py
+++ b/solution.py
@@ -185,9 +185,9 @@
 def fused_kernel(
     narrow, chips, hist, back,
     hl_hbm, ms_hbm, b_hbm, v_hbm, w_hbm, d_hbm, ot_hbm, ratio_ref, peak_ref,
-    hl_ref, ms_ref, b_ref, v_ref, w_ref, fw, cv, cw, ccl, hv, hw, ow, tp, tb, nm, cb, cnt, sq, sb, tot, tt, sc, scb, rt, mrow, mb, dm, de, ot_ref,
+    hl_ref, ms_ref, b_ref, v_ref, w_ref, fw, cv, cw, ccl, hv, hw, ow, tp, tb, nm, cb, cnt, sq, sb, tot, tt, bf, bo, bm, sc, scb, rt, mrow, mb, dm, de, ot_ref,
     rdy_s, ax_s, ax_r, ha_s, ha_r, fw_s, fw_r, hw_s, hw_r, ow_s, ow_r, tp_s, tp_r, cb_s, cb_r, ct_s, ct_r,
-    sq_s, sq_r, tt_s, tt_r, sc_s, sc_r, mx_s, mx_r, or_s, or_r, op_s, op_r, lc,
+    sq_s, sq_r, tt_s, tt_r, sc_s, sc_r, mx_s, mx_r, or_s, or_r, op_s, op_r, bf_s, bf_r, lc,
 ):
     me = lax.axis_index("wide") * narrow + lax.axis_index("narrow")
     q, c = lax.div(me, 2), lax.rem(me, 2)
@@ -330,7 +330,7 @@
         return remote(hv.at[:, cols(s)], hv.at[:, cols(s)], fw_s.at[0], ha_r.at[s], q + 2 * back, c)
 
     most = slots // 2
-    first = slots * 3 // 4
+    first = slots * 4 // 8
 
     def start_early(when, low, high, to):
         @pl.when(when)
@@ -351,6 +351,9 @@
     late_sends = jnp.logical_and(is_late, sends_early)
     late_direct = jnp.logical_and(late_sends, jnp.logical_not(late_splits))
     via = 1
+    odd = lax.rem(q, 2) == 1
+    odd_sends = jnp.logical_and(late_sends, odd)
+    even_sends = jnp.logical_and(late_sends, jnp.logical_not(odd))
 
     def early_via(h, i):
         return remote(v_ref.at[:, half_col(h, most + i)], fw.at[mine, cols(i)], ha_s.at[0], fw_r.at[i], q - back, h)
@@ -490,6 +493,7 @@
         cross_coeffs(q - hist).start()
         start_early(late_direct, most, most + via, q + back)
         start_early(late_sends, most + via, slots - 1, q + back)
+        start_early(even_sends, slots - 1, slots, q + back)
 
         @pl.when(late_splits)
         def _():
@@ -520,7 +524,7 @@
     def _():
         send_total.start()
 
-    start_early(late_sends, slots - 1, slots, q + back)
+    start_early(odd_sends, slots - 1, slots, q + back)
 
     def send_squares(s):
         return remote(sq.at[s], sb.at[q], sq_s.at[0], sq_r.at[0], hist + s, c)
@@ -545,7 +549,9 @@
         return remote(rt.at[theirs, cols(s)], ratio_ref.at[:, half_col(c, s)], or_s.at[0], or_r.at[0], q, 1 - c)
 
     def peak_out(s):
-        return remote(hv.at[theirs, cols(s)], peak_ref.at[:, half_col(c, s)], op_s.at[0], op_r.at[0], q, 1 - c)
+        return remote(ccl.at[theirs, cols(s)], peak_ref.at[:, half_col(c, s)], op_s.at[0], op_r.at[0], q, 1 - c)
+
+    give_before = remote(bf, bo, bf_s.at[0], bf_r.at[0], q, 1 - c)
 
     @pl.when(is_late)
     def _():
@@ -614,23 +620,35 @@
             rt[:, cols(s)] = scaled
             ratio_out(s).start()
             ratio_ref[:, half_col(c, s)] = rt[mine, cols(s)]
+            ccl[:, cols(s)] = ccl[:, cols(s)] * scb[s]
+            peak_out(s).start()
+
+        bm[...] = jnp.zeros_like(bm)
 
         @pl.loop(0, q - hist)
         def _(k):
             drain(mrow, mx_r.at[k])
+            bm[...] = jnp.maximum(bm[...], mb[k])
+
+        for s in range(slots):
+            bf[0:1, s * own : (s + 1) * own] = bm[s] * scb[s]
+
+        give_before.start()
 
         @pl.loop(0, slots)
         def _(s):
-            def earlier(k, best):
-                return jnp.maximum(best, mb[k, s])
-
-            before = lax.fori_loop(0, q - hist, earlier, jnp.zeros((1, own), jnp.float32))
-            hv[:, cols(s)] = jnp.maximum(ccl[:, cols(s)], before) * scb[s]
-            peak_out(s).start()
-            peak_ref[:, half_col(c, s)] = hv[mine, cols(s)]
+            peak_ref[:, half_col(c, s)] = jnp.maximum(ccl[mine, cols(s)], bf[0:1, cols(s)])
 
         drain(ratio_ref.at[:, other_half], or_r.at[0])
         drain(peak_ref.at[:, other_half], op_r.at[0])
+        give_before.wait_recv()
+
+        @pl.loop(0, slots)
+        def _(s):
+            other = half_col(1 - c, s)
+            peak_ref[:, other] = jnp.maximum(peak_ref[:, other], bo[0:1, cols(s)])
+
+        give_before.wait_send()
         drain(ratio_ref.at[:, other_half], or_s.at[0])
         drain(peak_ref.at[:, other_half], op_s.at[0])
 
@@ -717,6 +735,9 @@
         pltpu.VMEM((hist, 1, own), f32),
         pltpu.VMEM((1, half), f32),
         pltpu.VMEM((1, half), f32),
+        pltpu.VMEM((1, half), f32),
+        pltpu.VMEM((1, half), f32),
+        pltpu.VMEM((hist, 1, own), f32),
         pltpu.VMEM((1, own), f32),
         pltpu.VMEM((late, 1, own), f32),
         pltpu.VMEM((chip_rows, half), f32),
@@ -734,7 +755,7 @@
     for number in (1, 1):
         scratch += [dma((number,)), dma((number,))]
     scratch += [dma((1,)), dma((1,))]
-    for number in (1, late, 1, 1):
+    for number in (1, late, 1, 1, 1):
         scratch += [dma((number,)), dma((number,))]
     scratch.append(dma((11,)))
     outs = pl.pallas_call(

time: 38.6 us -> 37.7 us (0.977); the launches traced: 38.5 us -> 37.2 us
  Pallas kernels: 36.5 us -> 35.2 us
    pallas_call x1, Pallas kernels: 35.2 us -> 33.9 us  [fused_device(): pl.pallas_call(functools.partial(fused_kernel, narrow, chips, hist, back)...]
where the time goes in v4:
time: 37.7 us; the launch traced here: 37.2 us
  Pallas kernels  35.2 us (93%)
  between operations  1.93 us (5%)
    pallas_call x1, Pallas kernels, fused_device(): pl.pallas_call(functools.partial(fused_kernel, narrow, chips, hist, back)...  33.9 us
    pallas_call x1, Pallas kernels, fused_device(): pl.pallas_call(store_kernel, out_shape=[jax.ShapeDtypeStruct((rows, pixel...  1.33 us

profile of v4, /device:TPU:31, one launch (start us, length us, event | category | flops | bytes accessed | tf_op | source)
XLA Modules:
  0.0 37.2 jit_solution(17071169082553302452)
XLA Ops:
  1.9 33.9 %shard_map.86 = (f32[16,16384]{1,0:T(8,128)S(1)}, f32[16,16384]{1,0:T(8,128)S(1)}) custom-call(s32[1]{0:T(128)S(6)} %copy.9.hl_hbm, s32[1]{0:T(128)S(6)} %copy.10.ms_hbm, s32[512]{0:T(512)} %b_hbm.1, f32[16,16384]{1,0:T(8,128)} %v_hbm.1, s32[16,512]{1,0:T(8,128)} %w_hbm.1, f32[16,32,8]{2,1,0:T(8,128)} %constant.4.clone.d_hbm, f32[40,256]{1,0:T(8,128)} %constant.5.clone.ot_hbm), custom_call_target="tpu_custom_call" | custom-call | tf_op jit(solution)/shard_map/pallas_call | solution.py:761
  35.8 1.3 %shard_map.87 = (f32[16,16384]{1,0:T(8,128)}, f32[16,16384]{1,0:T(8,128)}) custom-call(f32[16,16384]{1,0:T(8,128)S(1)} %get-tuple-element.4.ratio_ref, f32[16,16384]{1,0:T(8,128)S(1)} %get-tuple-element.5.peak_ref), custom_call_target="tpu_custom_call" | custom-call | tf_op jit(solution)/shard_map/pallas_call | solution.py:772

commit v5 on v4

--- a/solution.py
+++ b/solution.py
@@ -331,6 +331,7 @@
 
     most = slots // 2
     first = slots * 4 // 8
+    ready = slots * 6 // 8
 
     def start_early(when, low, high, to):
         @pl.when(when)
@@ -351,7 +352,7 @@
     late_sends = jnp.logical_and(is_late, sends_early)
     late_direct = jnp.logical_and(late_sends, jnp.logical_not(late_splits))
     via = 1
-    odd = lax.rem(q, 2) == 1
+    odd = jnp.logical_and(lax.rem(q, 2) == 1, q + back + 1 < chips)
     odd_sends = jnp.logical_and(late_sends, odd)
     even_sends = jnp.logical_and(late_sends, jnp.logical_not(odd))
 
@@ -599,6 +600,10 @@
         def _(k):
             send_scale(k).start()
 
+        @pl.loop(first, ready)
+        def _(s):
+            rt[:, cols(s)] = window(s)
+
         send_total.wait_recv()
 
         @pl.loop(0, first)
@@ -607,7 +612,11 @@
 
         send_maxima(0)
 
-        @pl.loop(first, slots)
+        @pl.loop(first, ready)
+        def _(s):
+            statistic(s, rt[:, cols(s)])
+
+        @pl.loop(ready, slots)
         def _(s):
             statistic(s, window(s))
 

time: 37.7 us -> 37.8 us (level)
  no operation moved by 1% of the time
where the time goes in v5:
time: 37.8 us; the launch traced here: 37.2 us
  Pallas kernels  35.2 us (93%)
  between operations  1.93 us (5%)
    pallas_call x1, Pallas kernels, fused_device(): pl.pallas_call(functools.partial(fused_kernel, narrow, chips, hist, back)...  33.9 us
    pallas_call x1, Pallas kernels, fused_device(): pl.pallas_call(store_kernel, out_shape=[jax.ShapeDtypeStruct((rows, pixel...  1.33 us

profile of v5, /device:TPU:31, one launch (start us, length us, event | category | flops | bytes accessed | tf_op | source)
XLA Modules:
  0.0 37.2 jit_solution(4667012115886336473)
XLA Ops:
  1.9 33.9 %shard_map.86 = (f32[16,16384]{1,0:T(8,128)S(1)}, f32[16,16384]{1,0:T(8,128)S(1)}) custom-call(s32[1]{0:T(128)S(6)} %copy.9.hl_hbm, s32[1]{0:T(128)S(6)} %copy.10.ms_hbm, s32[512]{0:T(512)} %b_hbm.1, f32[16,16384]{1,0:T(8,128)} %v_hbm.1, s32[16,512]{1,0:T(8,128)} %w_hbm.1, f32[16,32,8]{2,1,0:T(8,128)} %constant.4.clone.d_hbm, f32[40,256]{1,0:T(8,128)} %constant.5.clone.ot_hbm), custom_call_target="tpu_custom_call" | custom-call | tf_op jit(solution)/shard_map/pallas_call | solution.py:770
  35.8 1.3 %shard_map.87 = (f32[16,16384]{1,0:T(8,128)}, f32[16,16384]{1,0:T(8,128)}) custom-call(f32[16,16384]{1,0:T(8,128)S(1)} %get-tuple-element.4.ratio_ref, f32[16,16384]{1,0:T(8,128)S(1)} %get-tuple-element.5.peak_ref), custom_call_target="tpu_custom_call" | custom-call | tf_op jit(solution)/shard_map/pallas_call | solution.py:781
